TPU v7x, 512 devices: a whole 4x4x16 slice. The times are simulated.
512 devices in a mesh: seq: 64 (over z_hi, y, x, core), head: 8 (over z_lo).
Axes of the slice: x: 4, y: 4, z: 16 (z_hi: 2, z_lo: 8; z = z_hi * 8 + z_lo), core: 2. Of those that a mesh axis runs over, the one named last changes fastest.
Arguments:
- queries: bfloat16 [49152, 128], P('seq'), may hold values from -6 to 6
- keys: bfloat16 [49152, 128], P('seq'), may hold values from -0.023925781 to 0.023925781
- values: bfloat16 [49152, 8192], P('seq', 'head'), may hold values from -6 to 6
- log_decay: float32 [128, 49152], P('head', 'seq'), may hold values from -0.8 to 0
- level_weight: bfloat16 [7, 128, 49152], P(None, 'head', 'seq'), may hold values from 0.099609375 to 1
- skip: float32 [128], P('head'), may hold values from 0.4 to 4.5
- norm_gain: bfloat16 [8192], P('head'), may hold values from 0.25 to 1.75
Outputs:
- normed: bfloat16 [49152, 8192], P('seq', 'head')
All inputs are finite; a program needn't handle non-finite values.
Results may differ from a plain program's by a relative error of at most 0.007.
Values sent between devices are 32-bit elements; how exact they have to be, the bound alone decides.
A program may use at most 128 MiB of HBM per device.

v0:
```python
import jax
import jax.numpy as jnp
from jax import lax
from jax.sharding import PartitionSpec as P


def partner(value, axis, stride):
    return lax.ppermute(value, axis, [(i, i ^ 1 << stride) for i in range(lax.axis_size(axis))])


def from_everyone(value, axis):
    peers = lax.axis_size(axis)
    return lax.all_to_all(
        jnp.broadcast_to(value[None], (peers, *value.shape)), axis, 0, 0, tiled=True
    )


def of_everyone(value, axis):
    return from_everyone(value, axis).sum(axis=0)


def split_project_all(queries, stacked):
    upper_part = stacked.astype(jnp.bfloat16)
    lower_part = (stacked - upper_part.astype(jnp.float32)).astype(jnp.bfloat16)
    first = jnp.einsum("tn,lhnp->lhtp", queries, upper_part, preferred_element_type=jnp.float32)
    second = jnp.einsum("tn,lhnp->lhtp", queries, lower_part, preferred_element_type=jnp.float32)
    return first + second


def shards(queries, keys, values, log_decay, level_weight, skip, norm_gain):
    tok_rows = queries.shape[0]
    head_count = log_decay.shape[0]
    chan_width = values.shape[1]
    head_size = chan_width // head_count
    decay_cum = jnp.cumsum(log_decay, axis=1)
    block_totals = decay_cum[:, -1]
    scores = jnp.dot(queries, keys.T, preferred_element_type=jnp.float32)
    position = jnp.arange(tok_rows, dtype=jnp.int32)
    causal = position[:, None] >= position[None, :]
    head_values = values.reshape(tok_rows, head_count, head_size).transpose(1, 0, 2)
    keys_f32 = keys.astype(jnp.float32)

    def head_terms(inputs):
        cum_head, head_vals = inputs
        spread_in = jnp.where(causal, cum_head[:, None] - cum_head[None, :], 0.0)
        mixing = (jnp.where(causal, jnp.exp(spread_in), 0.0) * scores).astype(jnp.bfloat16)
        inner = jnp.dot(mixing, head_vals, preferred_element_type=jnp.float32)
        scaled_keys = (keys_f32 * jnp.exp(cum_head[-1] - cum_head)[:, None]).astype(jnp.bfloat16)
        head_state = jnp.einsum(
            "sn,sp->np", scaled_keys, head_vals, preferred_element_type=jnp.float32
        )
        return (inner, head_state)

    inner_all, states = lax.map(head_terms, (decay_cum, head_values))
    weights_f32 = level_weight.astype(jnp.float32)
    mixed_out = weights_f32[0][:, :, None] * inner_all + skip[:, None, None] * head_values.astype(
        jnp.float32
    )
    level_count = lax.axis_size("seq").bit_length() - 1
    seq_index = lax.axis_index("seq")
    group_state = states
    group_total = block_totals
    offset = jnp.zeros_like(block_totals)
    buckets = []
    coef_list = []
    for level_no in range(level_count):
        level_bit = seq_index // (1 << level_no) % 2
        level_flag = level_bit.astype(jnp.float32)
        partner_state, partner_total = partner((group_state, group_total), "seq", level_no)
        level_coef = weights_f32[level_no + 1] * level_flag * jnp.exp(decay_cum + offset[:, None])
        buckets.append(partner_state)
        coef_list.append(level_coef)
        if level_no + 1 < level_count:
            left_state = jnp.where(level_bit == 1, partner_state, group_state)
            right_state = jnp.where(level_bit == 1, group_state, partner_state)
            right_total = jnp.where(level_bit == 1, group_total, partner_total)
            group_state = jnp.exp(right_total)[:, None, None] * left_state + right_state
        offset = offset + level_flag * partner_total
        group_total = group_total + partner_total
    stacked = jnp.stack(buckets)
    projected_all = split_project_all(queries, stacked)
    coef_all = jnp.stack(coef_list)
    mixed_out = mixed_out + jnp.sum(coef_all[:, :, :, None] * projected_all, axis=0)
    local_squares = jnp.sum(mixed_out * mixed_out, axis=(0, 2))
    sum_squares = of_everyone(local_squares, "head")
    inv_rms = lax.rsqrt(sum_squares / (head_count * head_size * lax.axis_size("head")) + 1e-05)
    scaled_out = mixed_out * inv_rms[None, :, None]
    result_rows = scaled_out.transpose(1, 0, 2).reshape(tok_rows, chan_width) * norm_gain.astype(
        jnp.float32
    )
    return result_rows.astype(jnp.bfloat16)


def solution(mesh):
    placed = (
        P("seq", None),
        P("seq", None),
        P("seq", "head"),
        P("head", "seq"),
        P(None, "head", "seq"),
        P("head"),
        P("head"),
    )
    return jax.shard_map(
        shards, mesh=mesh, in_specs=placed, out_specs=P("seq", "head"), check_vma=False
    )
```

profile of v0, /device:TPU:4, one launch (start us, length us, event | category | flops | bytes accessed | tf_op | source)
XLA Modules:
  0.0 257.2 jit_solution(13017375326448323190)
XLA Ops:
  6.5 72.8 %while.14 = (s32[]{:T(128)}, f32[16,768,64]{1,2,0:T(8,128)}, f32[16,128,64]{1,2,0:T(8,128)S(1)}, f32[16,768]{1,0:T(8,128)S(1)}, f32[768,768]{1,0:T(8,128)}, /*in...) while((s32[]{:T(128)}, f32[16,768,64]{1,2,0:T(8,128)}, ...), condition=%wide.region_3.4_spmd.clone.clone, body=%wide.region_2.3_spmd.clone.clone.sunk | while | flops 91816704 | bytes 3205253 | solution.py:54
  12.6 3.0 %fusion.65 = f32[16,768,64]{1,2,0:T(8,128)} fusion(f32[16,768,64]{1,2,0:T(8,128)} %get-tuple-element.201, s32[]{:T(128)} %get-tuple-element.200, f32[768,768]{1,0:T(8,128)} %get-tuple-element.214, f32[768]{0:T(1024)S(1)} %dynamic-slice_reduce_fusion.2, bf16[16,768,64]{1,2,0:T(8,128)(2,1)S(1)} %get-tuple-element.215), kind=kOutput, calls=%fused_computation.9.clone.1 | convolution fusion | flops 79036416 | bytes 2663424 | tf_op jit(solution)/shard_map/while/body/eval_jaxpr/dot_general | solution.py:47
  26.3 3.0 %fusion.65 = f32[16,768,64]{1,2,0:T(8,128)} fusion(f32[16,768,64]{1,2,0:T(8,128)} %get-tuple-element.201, s32[]{:T(128)} %get-tuple-element.200, f32[768,768]{1,0:T(8,128)} %get-tuple-element.214, f32[768]{0:T(1024)S(1)} %dynamic-slice_reduce_fusion.2, bf16[16,768,64]{1,2,0:T(8,128)(2,1)S(1)} %get-tuple-element.215), kind=kOutput, calls=%fused_computation.9.clone.1 | convolution fusion | flops 79036416 | bytes 2663424 | tf_op jit(solution)/shard_map/while/body/eval_jaxpr/dot_general | solution.py:47
  30.8 3.0 %fusion.65 = f32[16,768,64]{1,2,0:T(8,128)} fusion(f32[16,768,64]{1,2,0:T(8,128)} %get-tuple-element.201, s32[]{:T(128)} %get-tuple-element.200, f32[768,768]{1,0:T(8,128)} %get-tuple-element.214, f32[768]{0:T(1024)S(1)} %dynamic-slice_reduce_fusion.2, bf16[16,768,64]{1,2,0:T(8,128)(2,1)S(1)} %get-tuple-element.215), kind=kOutput, calls=%fused_computation.9.clone.1 | convolution fusion | flops 79036416 | bytes 2663424 | tf_op jit(solution)/shard_map/while/body/eval_jaxpr/dot_general | solution.py:47
  44.5 3.0 %fusion.65 = f32[16,768,64]{1,2,0:T(8,128)} fusion(f32[16,768,64]{1,2,0:T(8,128)} %get-tuple-element.201, s32[]{:T(128)} %get-tuple-element.200, f32[768,768]{1,0:T(8,128)} %get-tuple-element.214, f32[768]{0:T(1024)S(1)} %dynamic-slice_reduce_fusion.2, bf16[16,768,64]{1,2,0:T(8,128)(2,1)S(1)} %get-tuple-element.215), kind=kOutput, calls=%fused_computation.9.clone.1 | convolution fusion | flops 79036416 | bytes 2663424 | tf_op jit(solution)/shard_map/while/body/eval_jaxpr/dot_general | solution.py:47
  49.0 3.0 %fusion.65 = f32[16,768,64]{1,2,0:T(8,128)} fusion(f32[16,768,64]{1,2,0:T(8,128)} %get-tuple-element.201, s32[]{:T(128)} %get-tuple-element.200, f32[768,768]{1,0:T(8,128)} %get-tuple-element.214, f32[768]{0:T(1024)S(1)} %dynamic-slice_reduce_fusion.2, bf16[16,768,64]{1,2,0:T(8,128)(2,1)S(1)} %get-tuple-element.215), kind=kOutput, calls=%fused_computation.9.clone.1 | convolution fusion | flops 79036416 | bytes 2663424 | tf_op jit(solution)/shard_map/while/body/eval_jaxpr/dot_general | solution.py:47
  62.7 3.0 %fusion.65 = f32[16,768,64]{1,2,0:T(8,128)} fusion(f32[16,768,64]{1,2,0:T(8,128)} %get-tuple-element.201, s32[]{:T(128)} %get-tuple-element.200, f32[768,768]{1,0:T(8,128)} %get-tuple-element.214, f32[768]{0:T(1024)S(1)} %dynamic-slice_reduce_fusion.2, bf16[16,768,64]{1,2,0:T(8,128)(2,1)S(1)} %get-tuple-element.215), kind=kOutput, calls=%fused_computation.9.clone.1 | convolution fusion | flops 79036416 | bytes 2663424 | tf_op jit(solution)/shard_map/while/body/eval_jaxpr/dot_general | solution.py:47
  71.8 3.0 %fusion.65 = f32[16,768,64]{1,2,0:T(8,128)} fusion(f32[16,768,64]{1,2,0:T(8,128)} %get-tuple-element.201, s32[]{:T(128)} %get-tuple-element.200, f32[768,768]{1,0:T(8,128)} %get-tuple-element.214, f32[768]{0:T(1024)S(1)} %dynamic-slice_reduce_fusion.2, bf16[16,768,64]{1,2,0:T(8,128)(2,1)S(1)} %get-tuple-element.215), kind=kOutput, calls=%fused_computation.9.clone.1 | convolution fusion | flops 79036416 | bytes 2663424 | tf_op jit(solution)/shard_map/while/body/eval_jaxpr/dot_general | solution.py:47
  76.3 3.0 %fusion.65 = f32[16,768,64]{1,2,0:T(8,128)} fusion(f32[16,768,64]{1,2,0:T(8,128)} %get-tuple-element.201, s32[]{:T(128)} %get-tuple-element.200, f32[768,768]{1,0:T(8,128)} %get-tuple-element.214, f32[768]{0:T(1024)S(1)} %dynamic-slice_reduce_fusion.2, bf16[16,768,64]{1,2,0:T(8,128)(2,1)S(1)} %get-tuple-element.215), kind=kOutput, calls=%fused_computation.9.clone.1 | convolution fusion | flops 79036416 | bytes 2663424 | tf_op jit(solution)/shard_map/while/body/eval_jaxpr/dot_general | solution.py:47
  85.8 3.1 %collective-permute-start.6 = (f32[16,128,64]{1,2,0:T(8,128)S(1)}, f32[16,128,64]{1,2,0:T(8,128)S(1)}, u32[]{:S(2)}, u32[]{:S(2)}) collective-permute-start(f32[16,128,64]{1,2,0:T(8,128)S(1)} %select_add_fusion.4), channel_id=1, source_target_pairs={{0,16},{8,24},{16,0},{24,8},{32,48},{40,56},{48,32},{56,40},{64,80... | collective-permute-start | bytes 1572872 | tf_op jit(solution)/shard_map/ppermute | solution.py:8
  92.3 9.7 %collective-permute-done.1 = f32[16]{0:T(128)S(1)} collective-permute-done((f32[16]{0:T(128)S(1)}, f32[16]{0:T(128)S(1)}, u32[]{:S(2)}, u32[]{:S(2)}) %collective-permute-start.1) | collective-permute-done | bytes 96 | tf_op jit(solution)/shard_map/ppermute | solution.py:8
  102.0 7.7 %collective-permute-start.2 = (f32[16]{0:T(128)S(1)}, f32[16]{0:T(128)S(1)}, u32[]{:S(2)}, u32[]{:S(2)}) collective-permute-start(f32[16]{0:T(128)S(1)} %get-tuple-element.142), channel_id=1, source_target_pairs={{0,32},{8,40},{16,48},{24,56},{32,0},{40,8},{48,16},{56,24},{64,96... | collective-permute-start | bytes 200 | tf_op jit(solution)/shard_map/ppermute | solution.py:8
  114.1 5.4 %collective-permute-start.7 = (f32[16,128,64]{1,2,0:T(8,128)}, f32[16,128,64]{1,2,0:T(8,128)S(1)}, u32[]{:S(2)}, u32[]{:S(2)}) collective-permute-start(f32[16,128,64]{1,2,0:T(8,128)} %select_add_fusion.3), channel_id=1, source_target_pairs={{0,32},{8,40},{16,48},{24,56},{32,0},{40,8},{48,16},{56,24},{64,96... | collective-permute-start | bytes 1572872 | tf_op jit(solution)/shard_map/ppermute | solution.py:8
  121.5 5.0 %collective-permute-done.4 = f32[16]{0:T(128)S(1)} collective-permute-done((f32[16]{0:T(128)S(1)}, f32[16]{0:T(128)S(1)}, u32[]{:S(2)}, u32[]{:S(2)}) %collective-permute-start.4) | collective-permute-done | bytes 96 | tf_op jit(solution)/shard_map/ppermute | solution.py:8
  131.2 3.6 %collective-permute-start.8 = (f32[16,128,64]{1,2,0:T(8,128)S(1)}, f32[16,128,64]{1,2,0:T(8,128)S(1)}, u32[]{:S(2)}, u32[]{:S(2)}) collective-permute-start(f32[16,128,64]{1,2,0:T(8,128)S(1)} %select_add_fusion.2), channel_id=1, source_target_pairs={{0,64},{8,72},{16,80},{24,88},{32,96},{40,104},{48,112},{56,120},{... | collective-permute-start | bytes 1572872 | tf_op jit(solution)/shard_map/ppermute | solution.py:8
  139.4 5.3 %collective-permute-done.8 = f32[16,128,64]{1,2,0:T(8,128)S(1)} collective-permute-done((f32[16,128,64]{1,2,0:T(8,128)S(1)}, f32[16,128,64]{1,2,0:T(8,128)S(1)}, u32[]{:S(2)}, u32[]{:S(2)}) %collective-permute-start.8) | collective-permute-done | bytes 524320 | tf_op jit(solution)/shard_map/ppermute | solution.py:8
  149.4 9.5 %collective-permute-done.9 = f32[16,128,64]{1,2,0:T(8,128)S(1)} collective-permute-done((f32[16,128,64]{1,2,0:T(8,128)S(1)}, f32[16,128,64]{1,2,0:T(8,128)S(1)}, u32[]{:S(2)}, u32[]{:S(2)}) %collective-permute-start.9) | collective-permute-done | bytes 524320 | tf_op jit(solution)/shard_map/ppermute | solution.py:8
  159.0 13.3 %collective-permute-start.10 = (f32[16,128,64]{1,2,0:T(8,128)S(1)}, f32[16,128,64]{1,2,0:T(8,128)S(1)}, u32[]{:S(2)}, u32[]{:S(2)}) collective-permute-start(f32[16,128,64]{1,2,0:T(8,128)S(1)} %select_add_fusion), channel_id=1, source_target_pairs={{0,256},{8,264},{16,272},{24,280},{32,288},{40,296},{48,304},{56,3... | collective-permute-start | bytes 1572872 | tf_op jit(solution)/shard_map/ppermute | solution.py:8
  172.4 11.9 %collective-permute-done.10 = f32[16,128,64]{1,2,0:T(8,128)S(1)} collective-permute-done((f32[16,128,64]{1,2,0:T(8,128)S(1)}, f32[16,128,64]{1,2,0:T(8,128)S(1)}, u32[]{:S(2)}, u32[]{:S(2)}) %collective-permute-start.10) | collective-permute-done | bytes 524320 | tf_op jit(solution)/shard_map/ppermute | solution.py:8
  184.4 8.0 %fusion.25 = f32[6,16,64,768]{3,2,1,0:T(8,128)} fusion(f32[6,16,128,64]{2,3,1,0:T(8,128)S(1)} %bitcast_dynamic-update-slice_fusion, bf16[768,128]{1,0:T(8,128)(2,1)S(1)} %copy-done), kind=kOutput, calls=%fused_computation.29 | convolution fusion | flops 1211105280 | bytes 22216704 | tf_op jit(solution)/shard_map/tn,lhnp->lhtp/dot_general | solution.py:26
  192.4 9.4 %multiply_reduce_fusion = f32[16,64,768]{2,1,0:T(8,128)S(1)} fusion(f32[6,16,64,768]{3,2,1,0:T(8,128)} %fusion.25, f32[6,16,768]{2,1,0:T(8,128)} %get-tuple-element.137, f32[6,16,128,64]{2,3,1,0:T(8,128)} %copy-done.1, bf16[768,128]{1,0:T(8,128)(2,1)S(1)} %copy-done), kind=kOutput, calls=%fused_computation.23 | convolution fusion | flops 1222115328 | bytes 25657344 | tf_op jit(solution)/shard_map/tn,lhnp->lhtp/dot_general | solution.py:25
  205.3 36.4 %all-to-all-start = ((f32[8,1,768]{2,1,0:T(1,128)}), f32[8,1,768]{2,1,0:T(1,128)S(1)}, u32[]{:S(2)}, u32[]{:S(2)}) async-start(f32[8,1,768]{2,1,0:T(1,128)} %broadcast_in_dim.24), calls=%async_computation | async-start | bytes 49152 | tf_op jit(solution)/shard_map/all_to_all | solution.py:13
  241.6 10.6 %all-to-all-done = f32[8,1,768]{2,1,0:T(1,128)S(1)} async-done(((f32[8,1,768]{2,1,0:T(1,128)}), f32[8,1,768]{2,1,0:T(1,128)S(1)}, u32[]{:S(2)}, u32[]{:S(2)}) %all-to-all-start) | async-done | bytes 24608 | tf_op jit(solution)/shard_map/all_to_all | solution.py:13
  252.2 3.1 %broadcast_multiply_fusion = f32[16,768,64]{1,2,0:T(8,128)S(1)} fusion(f32[768]{0:T(1024)S(1)} %add_rsqrt_fusion, f32[16,64,768]{2,1,0:T(8,128)S(1)} %multiply_reduce_fusion, f32[16]{0:T(128)S(1)} %copy-done.9, f32[16,768,64]{1,2,0:T(8,128)} %get-tuple-element.51, f32[16,768]{1,0:T(8,128)S(1)} %get-tuple-element.136, bf16[768,1024]{0,1:T(8,128)(2,1)} %bitcast.78), kind=kLoop, calls=%fused_computation.30 | loop fusion | flops 4718592 | bytes 11062336 | tf_op jit(solution)/shard_map/mul | solution.py:87
  (148 shorter events, 90.8 us)
Async XLA Ops:
  0.0 4.6 %copy-start = (bf16[768,128]{1,0:T(8,128)(2,1)S(1)}, bf16[768,128]{1,0:T(8,128)(2,1)}, u32[]{:S(2)}) copy-start(bf16[768,128]{1,0:T(8,128)(2,1)} %param.9) | copy-start | bytes 589828
  0.0 4.6 %copy-start.5 = (bf16[768,128]{1,0:T(8,128)(2,1)S(1)}, bf16[768,128]{1,0:T(8,128)(2,1)}, u32[]{:S(2)}) copy-start(bf16[768,128]{1,0:T(8,128)(2,1)} %param.10) | copy-start | bytes 589828
  6.5 77.5 %copy-start.7 = (bf16[7,16,768]{2,1,0:T(8,128)(2,1)S(1)}, bf16[7,16,768]{2,1,0:T(8,128)(2,1)}, u32[]{:S(2)}) copy-start(bf16[7,16,768]{2,1,0:T(8,128)(2,1)} %param.13) | copy-start | bytes 516100
  79.3 5.3 %copy-start.6 = (f32[16,128,64]{1,2,0:T(8,128)}, f32[16,128,64]{1,2,0:T(8,128)S(1)}, u32[]{:S(2)}) copy-start(f32[16,128,64]{1,2,0:T(8,128)S(1)} %get-tuple-element.52) | copy-start | bytes 1572868
  79.3 57.0 %copy-start.2 = (bf16[16,768,64]{1,2,0:T(8,128)(2,1)}, bf16[16,768,64]{1,2,0:T(8,128)(2,1)S(1)}, u32[]{:S(2)}) copy-start(bf16[16,768,64]{1,2,0:T(8,128)(2,1)S(1)} %get-tuple-element.220) | copy-start | bytes 4718596
  79.3 5.3 %collective-permute-start.5 = (f32[16,128,64]{1,2,0:T(8,128)S(1)}, f32[16,128,64]{1,2,0:T(8,128)S(1)}, u32[]{:S(2)}, u32[]{:S(2)}) collective-permute-start(f32[16,128,64]{1,2,0:T(8,128)S(1)} %get-tuple-element.52), channel_id=1, source_target_pairs={{0,8},{8,0},{16,24},{24,16},{32,40},{40,32},{48,56},{56,48},{64,72... | collective-permute-start | bytes 1572872 | tf_op jit(solution)/shard_map/ppermute | solution.py:8
  81.4 3.2 %collective-permute-start = (f32[16]{0:T(128)S(1)}, f32[16]{0:T(128)S(1)}, u32[]{:S(2)}, u32[]{:S(2)}) collective-permute-start(f32[16]{0:T(128)S(1)} %slice_reduce_fusion.1), channel_id=1, source_target_pairs={{0,8},{8,0},{16,24},{24,16},{32,40},{40,32},{48,56},{56,48},{64,72... | collective-permute-start | bytes 200 | tf_op jit(solution)/shard_map/ppermute | solution.py:8
  84.0 4.9 %copy-start.4 = (f32[7,16,768]{2,1,0:T(8,128)}, f32[7,16,768]{2,1,0:T(8,128)S(1)}, u32[]{:S(2)}) copy-start(f32[7,16,768]{2,1,0:T(8,128)S(1)} %convert_element_type.48) | copy-start | bytes 1032196
  85.8 27.4 %collective-permute-start.6 = (f32[16,128,64]{1,2,0:T(8,128)S(1)}, f32[16,128,64]{1,2,0:T(8,128)S(1)}, u32[]{:S(2)}, u32[]{:S(2)}) collective-permute-start(f32[16,128,64]{1,2,0:T(8,128)S(1)} %select_add_fusion.4), channel_id=1, source_target_pairs={{0,16},{8,24},{16,0},{24,8},{32,48},{40,56},{48,32},{56,40},{64,80... | collective-permute-start | bytes 1572872 | tf_op jit(solution)/shard_map/ppermute | solution.py:8
  89.6 12.4 %collective-permute-start.1 = (f32[16]{0:T(128)S(1)}, f32[16]{0:T(128)S(1)}, u32[]{:S(2)}, u32[]{:S(2)}) collective-permute-start(f32[16]{0:T(128)S(1)} %get-tuple-element.144), channel_id=1, source_target_pairs={{0,16},{8,24},{16,0},{24,8},{32,48},{40,56},{48,32},{56,40},{64,80... | collective-permute-start | bytes 200 | tf_op jit(solution)/shard_map/ppermute | solution.py:8
  102.0 9.3 %collective-permute-start.2 = (f32[16]{0:T(128)S(1)}, f32[16]{0:T(128)S(1)}, u32[]{:S(2)}, u32[]{:S(2)}) collective-permute-start(f32[16]{0:T(128)S(1)} %get-tuple-element.142), channel_id=1, source_target_pairs={{0,32},{8,40},{16,48},{24,56},{32,0},{40,8},{48,16},{56,24},{64,96... | collective-permute-start | bytes 200 | tf_op jit(solution)/shard_map/ppermute | solution.py:8
  111.3 8.3 %collective-permute-start.3 = (f32[16]{0:T(128)S(1)}, f32[16]{0:T(128)S(1)}, u32[]{:S(2)}, u32[]{:S(2)}) collective-permute-start(f32[16]{0:T(128)S(1)} %get-tuple-element.140), channel_id=1, source_target_pairs={{0,64},{8,72},{16,80},{24,88},{32,96},{40,104},{48,112},{56,120},{... | collective-permute-start | bytes 200 | tf_op jit(solution)/shard_map/ppermute | solution.py:8
  114.1 16.0 %collective-permute-start.7 = (f32[16,128,64]{1,2,0:T(8,128)}, f32[16,128,64]{1,2,0:T(8,128)S(1)}, u32[]{:S(2)}, u32[]{:S(2)}) collective-permute-start(f32[16,128,64]{1,2,0:T(8,128)} %select_add_fusion.3), channel_id=1, source_target_pairs={{0,32},{8,40},{16,48},{24,56},{32,0},{40,8},{48,16},{56,24},{64,96... | collective-permute-start | bytes 1572872 | tf_op jit(solution)/shard_map/ppermute | solution.py:8
  119.6 7.0 %collective-permute-start.4 = (f32[16]{0:T(128)S(1)}, f32[16]{0:T(128)S(1)}, u32[]{:S(2)}, u32[]{:S(2)}) collective-permute-start(f32[16]{0:T(128)S(1)} %get-tuple-element.138), channel_id=1, source_target_pairs={{0,128},{8,136},{16,144},{24,152},{32,160},{40,168},{48,176},{56,1... | collective-permute-start | bytes 200 | tf_op jit(solution)/shard_map/ppermute | solution.py:8
  131.2 13.4 %collective-permute-start.8 = (f32[16,128,64]{1,2,0:T(8,128)S(1)}, f32[16,128,64]{1,2,0:T(8,128)S(1)}, u32[]{:S(2)}, u32[]{:S(2)}) collective-permute-start(f32[16,128,64]{1,2,0:T(8,128)S(1)} %select_add_fusion.2), channel_id=1, source_target_pairs={{0,64},{8,72},{16,80},{24,88},{32,96},{40,104},{48,112},{56,120},{... | collective-permute-start | bytes 1572872 | tf_op jit(solution)/shard_map/ppermute | solution.py:8
  144.8 14.0 %collective-permute-start.9 = (f32[16,128,64]{1,2,0:T(8,128)S(1)}, f32[16,128,64]{1,2,0:T(8,128)S(1)}, u32[]{:S(2)}, u32[]{:S(2)}) collective-permute-start(f32[16,128,64]{1,2,0:T(8,128)S(1)} %select_add_fusion.1), channel_id=1, source_target_pairs={{0,128},{8,136},{16,144},{24,152},{32,160},{40,168},{48,176},{56,1... | collective-permute-start | bytes 1572872 | tf_op jit(solution)/shard_map/ppermute | solution.py:8
  159.0 25.3 %collective-permute-start.10 = (f32[16,128,64]{1,2,0:T(8,128)S(1)}, f32[16,128,64]{1,2,0:T(8,128)S(1)}, u32[]{:S(2)}, u32[]{:S(2)}) collective-permute-start(f32[16,128,64]{1,2,0:T(8,128)S(1)} %select_add_fusion), channel_id=1, source_target_pairs={{0,256},{8,264},{16,272},{24,280},{32,288},{40,296},{48,304},{56,3... | collective-permute-start | bytes 1572872 | tf_op jit(solution)/shard_map/ppermute | solution.py:8
  184.4 8.0 %copy-start.1 = (f32[6,16,128,64]{2,3,1,0:T(8,128)}, f32[6,16,128,64]{2,3,1,0:T(8,128)S(1)}, u32[]{:S(2)}) copy-start(f32[6,16,128,64]{2,3,1,0:T(8,128)S(1)} %bitcast_dynamic-update-slice_fusion) | copy-start | bytes 9437188
  192.4 9.4 %copy-start.3 = (bf16[16,768,64]{1,2,0:T(8,128)(2,1)S(1)}, bf16[16,768,64]{1,2,0:T(8,128)(2,1)}, u32[]{:S(2)}) copy-start(bf16[16,768,64]{1,2,0:T(8,128)(2,1)} %copy-done.2) | copy-start | bytes 4718596
  192.4 9.4 %copy-start.9 = (f32[16]{0:T(128)S(1)}, f32[16]{0:T(128)}, u32[]{:S(2)}) copy-start(f32[16]{0:T(128)} %param.14) | copy-start | bytes 196
  201.8 39.8 %copy-start.8 = (bf16[1024]{0:T(1024)(128)(2,1)S(1)}, bf16[1024]{0:T(1024)(128)(2,1)}, u32[]{:S(2)}) copy-start(bf16[1024]{0:T(1024)(128)(2,1)} %param.15) | copy-start | bytes 6148
  205.3 46.9 %all-to-all-start = ((f32[8,1,768]{2,1,0:T(1,128)}), f32[8,1,768]{2,1,0:T(1,128)S(1)}, u32[]{:S(2)}, u32[]{:S(2)}) async-start(f32[8,1,768]{2,1,0:T(1,128)} %broadcast_in_dim.24), calls=%async_computation | async-start | bytes 49152 | tf_op jit(solution)/shard_map/all_to_all | solution.py:13
where the time goes:
time: 259 us; the launch traced here: 257 us
  starting transfers between devices  83.4 us (32%)
  matrix products  71.9 us (28%)
  waiting for transfers between devices  56 us (22%)
  other arithmetic  29.9 us (12%)
  local copies, waits for them, and re-layouts  15.4 us (6%)
    dot_general x16, matrix products, head_terms(): inner = jnp.dot(mixing, head_vals, preferred_element_type=jnp.float32)  47.8 us
    ppermute x11, starting transfers between devices, partner(): lax.ppermute(value, axis, [(i, i ^ 1 << stride) for i in range(lax.axis_s...  47 us
    ppermute x11, waiting for transfers between devices, partner(): lax.ppermute(value, axis, [(i, i ^ 1 << stride) for i in range(lax.axis_s...  45.5 us
    all_to_all x1, starting transfers between devices, from_everyone(): lax.all_to_all(jnp.broadcast_to(value[None], (peers, *value.shape)), axis...  36.4 us
    all_to_all x1, waiting for transfers between devices, from_everyone(): lax.all_to_all(jnp.broadcast_to(value[None], (peers, *value.shape)), axis...  10.6 us
    exp x16, other arithmetic, head_terms(): jnp.exp(cum_head[-1] - cum_head)[:, None]  10 us
    slice x16, local copies, waits for them, and re-layouts, head_terms(): cum_head[-1] - cum_head  9.64 us
    dot_general x1, matrix products, split_project_all(): jnp.einsum('tn,lhnp->lhtp', queries, upper_part, preferred_element_type=j...  9.37 us
  transfers between devices with their start and end apart: 12, of which 9 were waited for; matrix products, arithmetic and copies ran while one was open for 4% of the time, Pallas kernels for 0%

commit v1 on v0

v1 whole, which is shorter than its diff:
```python
import jax
import jax.numpy as jnp
from jax import lax
from jax.experimental import pallas as pl
from jax.experimental.pallas import tpu as pltpu
from jax.sharding import PartitionSpec as P

F32 = jnp.float32
BF16 = jnp.bfloat16
NT = (((1,), (1,)), ((), ()))

TOK = 768
CH = 128
NC = TOK // CH
HEADS = 16
DIM = 64
STATE = 128
ROWS = HEADS * DIM
HALF = ROWS // 2
PLANE = 32
CHIPS = 16
SLICE = HALF // CHIPS
LEVELS = 6
GROUP = 8
CHANNELS = 8192


def rows_of(start, size):
    return pl.ds(pl.multiple_of(start, SLICE), size)


def kernel(
    q_ref, k_ref, v_ref, ld_ref, lw_ref, skip_ref, gain_ref, out_ref,
    lc_ref, lct_ref, w0_ref, ci_ref, cum_ref, coef_ref, vt_ref, rb_ref, st_ref, acc_ref,
    tot_ref, tots_ref, gath_ref, node_ref, bucket_ref, zin_ref, bb_ref, sq_ref, sqs_ref,
    tot_ss, tot_rs, p1_ss, p1_rs, l0_ss, l0_rs, p2_ss, p2_rs, z_ss, z_rs, fw_ss, fw_rs, sq_ss, sq_rs,
):
    seq = lax.axis_index("seq")
    head = lax.axis_index("head")
    zhi = seq // PLANE
    me = seq % PLANE
    chip = me // 2
    core = me % 2
    base = zhi * PLANE

    def at(s):
        return {"seq": s, "head": head}

    def remote(src, dst, ss, rs, device):
        return pltpu.make_async_remote_copy(
            src_ref=src, dst_ref=dst, send_sem=ss, recv_sem=rs,
            device_id=device, device_id_type=pl.DeviceIdType.MESH,
        )

    partner = at(base + me + 1 - 2 * core)
    zpeer = at(seq + PLANE - 2 * PLANE * zhi)

    barrier = pltpu.get_barrier_semaphore()

    @pl.loop(1, PLANE)
    def _(r):
        pl.semaphore_signal(
            barrier, inc=1, device_id=at(base + (me + r) % PLANE),
            device_id_type=pl.DeviceIdType.MESH)

    @pl.loop(1, GROUP)
    def _(r):
        pl.semaphore_signal(
            barrier, inc=1, device_id={"seq": seq, "head": (head + r) % GROUP},
            device_id_type=pl.DeviceIdType.MESH)

    @pl.when(zhi == 1)
    def _():
        pl.semaphore_signal(
            barrier, inc=1, device_id=zpeer, device_id_type=pl.DeviceIdType.MESH)

    row = lax.broadcasted_iota(jnp.int32, (CH, CH), 0)
    col = lax.broadcasted_iota(jnp.int32, (CH, CH), 1)
    tri = jnp.where(row <= col, 1.0, 0.0).astype(BF16)
    his, mids, los = [], [], []
    for c in range(NC):
        x = ld_ref[:, c * CH:(c + 1) * CH]
        hi = x.astype(BF16)
        rest = x - hi.astype(F32)
        mid = rest.astype(BF16)
        his.append(hi)
        mids.append(mid)
        los.append((rest - mid.astype(F32)).astype(BF16))
    sums = jnp.dot(jnp.concatenate(his + mids + los, axis=0), tri, preferred_element_type=F32)
    n = HEADS * NC
    total = jnp.zeros((HEADS, CH), F32)
    for c in range(NC):
        a = HEADS * c
        lc = sums[a:a + HEADS] + sums[n + a:n + a + HEADS] + sums[2 * n + a:2 * n + a + HEADS]
        lc_ref[c] = lc
        cum_ref[c] = lc + total
        padded = jnp.concatenate([lc, jnp.zeros((CH - HEADS, CH), F32)], axis=0)
        lct_ref[c] = padded.T
        w0 = lw_ref[0, :, c * CH:(c + 1) * CH].astype(F32)
        w0_ref[c] = w0
        ci_ref[c] = w0 * jnp.exp(lc)
        total = total + jnp.broadcast_to(lc[:, CH - 1:CH], (HEADS, CH))
    tot_ref[...] = total
    tots_ref[me] = total

    st_ref[...] = jnp.zeros((ROWS, STATE), F32)

    @pl.loop(0, NC)
    def _(c):
        lc = lc_ref[c]
        last = jnp.broadcast_to(lc[:, CH - 1:CH], (HEADS, CH))
        fall = jnp.exp(last)
        tail = jnp.exp(last - lc)
        scaled = []
        for j in range(ROWS // CH):
            vt = v_ref[c, :, j * CH:(j + 1) * CH].T
            vt_ref[c, j * CH:(j + 1) * CH, :] = vt
            wide = vt.astype(F32)
            for i in range(2):
                h = 2 * j + i
                scaled.append((wide[i * DIM:(i + 1) * DIM] * tail[h:h + 1]).astype(BF16))
        new = jnp.dot(jnp.concatenate(scaled, axis=0), k_ref[c], preferred_element_type=F32)
        for h in range(HEADS):
            rows = slice(h * DIM, (h + 1) * DIM)
            old = st_ref[rows]
            rb_ref[c, rows] = old.astype(BF16)
            st_ref[rows] = fall[h:h + 1] * old + new[rows]

    pl.semaphore_wait(barrier, PLANE - 1 + GROUP - 1 + 1 - zhi)

    @pl.when(core == 0)
    def _():
        remote(st_ref, bucket_ref.at[0], l0_ss, l0_rs, partner).start()

    @pl.loop(1, PLANE)
    def _(r):
        to = (me + r) % PLANE
        dev = at(base + to)
        remote(tot_ref, tots_ref.at[me], tot_ss, tot_rs, dev).start()
        own = HALF * (to % 2) + SLICE * (to // 2)
        remote(st_ref.at[rows_of(own, SLICE)], gath_ref.at[me], p1_ss, p1_rs, dev).start()

    mine = HALF * core + SLICE * chip
    gath_ref[me] = st_ref[rows_of(mine, SLICE)]

    @pl.loop(0, NC)
    def _(c):
        qc = q_ref[c]
        s = lax.dot_general(k_ref[c], qc, NT, preferred_element_type=F32)
        r0 = lax.broadcasted_iota(jnp.int32, (CH, CH), 0)
        c0 = lax.broadcasted_iota(jnp.int32, (CH, CH), 1)
        s = jnp.where(r0 <= c0, s, 0.0)
        inter = lax.dot_general(rb_ref[c], qc, NT, preferred_element_type=F32)
        for h in range(HEADS):
            rows = slice(h * DIM, (h + 1) * DIM)
            d = jnp.minimum(lc_ref[c, h:h + 1] - lct_ref[c, :, h:h + 1], 0.0)
            mix = (jnp.exp(d) * s).astype(BF16)
            vt = vt_ref[c, rows]
            o = jnp.dot(vt, mix, preferred_element_type=F32)
            acc_ref[c, rows] = (
                w0_ref[c, h:h + 1] * o + ci_ref[c, h:h + 1] * inter[rows]
                + skip_ref[h] * vt.astype(F32))

    remote(tots_ref.at[pl.ds(0, PLANE - 1)], tots_ref.at[pl.ds(0, PLANE - 1)], tot_ss, tot_rs,
           partner).wait_recv()
    remote(gath_ref.at[pl.ds(0, PLANE - 1)], gath_ref.at[pl.ds(0, PLANE - 1)], p1_ss, p1_rs,
           partner).wait_recv()
    hd = 8 * core + chip // 2
    nodes = [gath_ref[i] for i in range(PLANE)]
    weights = [tots_ref[i, pl.ds(hd, 1), :] for i in range(PLANE)]
    slot = 0
    for level in range(1, LEVELS):
        joined = [
            jnp.exp(weights[2 * j + 1]) * nodes[2 * j] + nodes[2 * j + 1]
            for j in range(len(nodes) // 2)
        ]
        weights = [weights[2 * j] + weights[2 * j + 1] for j in range(len(nodes) // 2)]
        nodes = joined
        for j in range(0, len(nodes), 2):
            node_ref[slot] = nodes[j]
            slot += 1
    starts = [0, 0, 8, 12, 14, 15]

    @pl.when(zhi == 0)
    def _():
        remote(node_ref.at[starts[5]], zin_ref, z_ss, z_rs, zpeer).start()

    bits = [core] + [(chip // (1 << b)) % 2 for b in range(4)] + [zhi]

    @pl.loop(1, CHIPS)
    def _(r):
        to = (chip + r) % CHIPS
        dev = at(base + 2 * to + core)
        for level in range(1, 5):
            @pl.when((to // (1 << (level - 1))) % 2 == 1)
            def _():
                remote(
                    node_ref.at[starts[level] + to // (1 << level)],
                    bucket_ref.at[level, rows_of(mine, SLICE)],
                    p2_ss.at[level - 1], p2_rs.at[level - 1], dev).start()

    for level in range(1, 5):
        @pl.when(bits[level] == 1)
        def _():
            bucket_ref[level, rows_of(mine, SLICE)] = node_ref[starts[level] + chip // (1 << level)]

    offs = [jnp.zeros((HEADS, CH), F32) for _ in range(LEVELS)]
    for i in range(PLANE - 1):
        t = tots_ref[i]
        for level in range(1, LEVELS):
            inside = (i < me) & (i >= me - me % (1 << level))
            offs[level] = offs[level] + jnp.where(inside, t, 0.0)
    for level in range(LEVELS):
        for c in range(NC):
            w = lw_ref[level + 1, :, c * CH:(c + 1) * CH].astype(F32)
            coef_ref[level, c] = w * jnp.exp(cum_ref[c] + offs[level])

    def cross(level):
        bb_ref[...] = bucket_ref[level].astype(BF16)

        @pl.loop(0, NC // 2)
        def _(d):
            q2 = q_ref[pl.ds(2 * d, 2)].reshape(2 * CH, STATE)
            o = lax.dot_general(bb_ref[...], q2, NT, preferred_element_type=F32)
            for i in range(2):
                c = 2 * d + i
                for h in range(HEADS):
                    rows = slice(h * DIM, (h + 1) * DIM)
                    acc_ref[c, rows] = (
                        acc_ref[c, rows]
                        + coef_ref[level, c, h:h + 1] * o[rows, i * CH:(i + 1) * CH])

    half = rows_of(HALF * core, HALF)
    other = rows_of(HALF * (1 - core), HALF)
    some = pl.ds(0, (CHIPS - 1) * SLICE)

    @pl.when(core == 1)
    def _():
        remote(st_ref, bucket_ref.at[0], l0_ss, l0_rs, partner).wait_recv()
        cross(0)

    for level in range(1, 5):
        @pl.when(bits[level] == 1)
        def _():
            remote(
                bucket_ref.at[level, some], bucket_ref.at[level, some],
                p2_ss.at[level - 1], p2_rs.at[level - 1], partner).wait_recv()
            remote(
                bucket_ref.at[level, half], bucket_ref.at[level, half],
                fw_ss.at[level - 1], fw_rs.at[level - 1], partner).start()

    @pl.when(zhi == 1)
    def _():
        remote(zin_ref, zin_ref, z_ss, z_rs, zpeer).wait_recv()

        @pl.loop(1, CHIPS)
        def _(r):
            to = (chip + r) % CHIPS
            remote(
                zin_ref, bucket_ref.at[5, rows_of(mine, SLICE)],
                p2_ss.at[4], p2_rs.at[4], at(base + 2 * to + core)).start()
        bucket_ref[5, rows_of(mine, SLICE)] = zin_ref[...]

    for level in range(1, 5):
        @pl.when(bits[level] == 1)
        def _():
            remote(
                bucket_ref.at[level, half], bucket_ref.at[level, other],
                fw_ss.at[level - 1], fw_rs.at[level - 1], partner).wait_recv()
            cross(level)

    @pl.when(zhi == 1)
    def _():
        remote(
            bucket_ref.at[5, some], bucket_ref.at[5, some],
            p2_ss.at[4], p2_rs.at[4], partner).wait_recv()
        remote(
            bucket_ref.at[5, half], bucket_ref.at[5, half],
            fw_ss.at[4], fw_rs.at[4], partner).start()
        remote(
            bucket_ref.at[5, half], bucket_ref.at[5, other],
            fw_ss.at[4], fw_rs.at[4], partner).wait_recv()
        cross(5)

    sq_ref[...] = jnp.zeros((8, CH), F32)
    for c in range(NC):
        y = acc_ref[c]
        sq_ref[c:c + 1] = jnp.sum(y * y, axis=0, keepdims=True)
    sqs_ref[head] = sq_ref[...]

    @pl.loop(1, GROUP)
    def _(r):
        remote(
            sq_ref, sqs_ref.at[head], sq_ss, sq_rs,
            {"seq": seq, "head": (head + r) % GROUP}).start()

    remote(tots_ref.at[pl.ds(0, PLANE - 1)], tots_ref.at[pl.ds(0, PLANE - 1)], tot_ss, tot_rs,
           partner).wait_send()
    remote(gath_ref.at[pl.ds(0, PLANE - 1)], gath_ref.at[pl.ds(0, PLANE - 1)], p1_ss, p1_rs,
           partner).wait_send()

    @pl.when(core == 0)
    def _():
        remote(st_ref, bucket_ref.at[0], l0_ss, l0_rs, partner).wait_send()

    for level in range(1, 5):
        for has in range(2):
            @pl.when(bits[level] == has)
            def _():
                some_sent = pl.ds(0, (CHIPS // 2 - has) * SLICE)
                remote(
                    bucket_ref.at[level, some_sent], bucket_ref.at[level, some_sent],
                    p2_ss.at[level - 1], p2_rs.at[level - 1], partner).wait_send()

        @pl.when(bits[level] == 1)
        def _():
            remote(
                bucket_ref.at[level, half], bucket_ref.at[level, half],
                fw_ss.at[level - 1], fw_rs.at[level - 1], partner).wait_send()

    @pl.when(zhi == 0)
    def _():
        remote(node_ref.at[starts[5]], zin_ref, z_ss, z_rs, zpeer).wait_send()

    @pl.when(zhi == 1)
    def _():
        remote(
            bucket_ref.at[5, some], bucket_ref.at[5, some],
            p2_ss.at[4], p2_rs.at[4], partner).wait_send()
        remote(
            bucket_ref.at[5, half], bucket_ref.at[5, half],
            fw_ss.at[4], fw_rs.at[4], partner).wait_send()

    seven = sqs_ref.at[pl.ds(0, GROUP - 1)]
    remote(seven, seven, sq_ss, sq_rs, partner).wait_recv()
    whole = sqs_ref[0]
    for g in range(1, GROUP):
        whole = whole + sqs_ref[g]
    remote(seven, seven, sq_ss, sq_rs, partner).wait_send()
    sq_ref[...] = lax.rsqrt(whole / CHANNELS + 1e-05)

    @pl.loop(0, NC)
    def _(c):
        inv = sq_ref[pl.ds(c, 1), :]
        for j in range(ROWS // CH):
            cols = slice(j * CH, (j + 1) * CH)
            y = (acc_ref[c, cols] * inv).T
            out_ref[c, :, cols] = (y * gain_ref[:, cols].astype(F32)).astype(BF16)


def shards(queries, keys, values, log_decay, level_weight, skip, norm_gain):
    vmem = pl.BlockSpec(memory_space=pltpu.VMEM)
    dma = pltpu.SemaphoreType.DMA
    out = pl.pallas_call(
        kernel,
        out_shape=jax.ShapeDtypeStruct((NC, CH, ROWS), BF16),
        in_specs=[vmem] * 5 + [pl.BlockSpec(memory_space=pltpu.SMEM), vmem],
        out_specs=vmem,
        scratch_shapes=[
            pltpu.VMEM((NC, HEADS, CH), F32),
            pltpu.VMEM((NC, CH, CH), F32),
            pltpu.VMEM((NC, HEADS, CH), F32),
            pltpu.VMEM((NC, HEADS, CH), F32),
            pltpu.VMEM((NC, HEADS, CH), F32),
            pltpu.VMEM((LEVELS, NC, HEADS, CH), F32),
            pltpu.VMEM((NC, ROWS, CH), BF16),
            pltpu.VMEM((NC, ROWS, STATE), BF16),
            pltpu.VMEM((ROWS, STATE), F32),
            pltpu.VMEM((NC, ROWS, CH), F32),
            pltpu.VMEM((HEADS, CH), F32),
            pltpu.VMEM((PLANE, HEADS, CH), F32),
            pltpu.VMEM((PLANE, SLICE, STATE), F32),
            pltpu.VMEM((CHIPS, SLICE, STATE), F32),
            pltpu.VMEM((LEVELS, ROWS, STATE), F32),
            pltpu.VMEM((SLICE, STATE), F32),
            pltpu.VMEM((ROWS, STATE), BF16),
            pltpu.VMEM((8, CH), F32),
            pltpu.VMEM((GROUP, 8, CH), F32),
            dma, dma, dma, dma, dma, dma, dma((5,)), dma((5,)), dma, dma, dma((5,)), dma((5,)),
            dma, dma,
        ],
        compiler_params=pltpu.CompilerParams(
            collective_id=0, has_side_effects=True, vmem_limit_bytes=50 << 20),
        name="layer",
    )(
        queries.reshape(NC, CH, STATE), keys.reshape(NC, CH, STATE), values.reshape(NC, CH, ROWS),
        log_decay, level_weight, skip, norm_gain.reshape(1, ROWS),
    )
    return out.reshape(TOK, ROWS)


def solution(mesh):
    placed = (
        P("seq", None), P("seq", None), P("seq", "head"), P("head", "seq"),
        P(None, "head", "seq"), P("head"), P("head"),
    )
    return jax.shard_map(
        shards, mesh=mesh, in_specs=placed, out_specs=P("seq", "head"), check_vma=False
    )
```

time: 259 us -> 59.8 us (0.23)
  the two profiles are of different devices: /device:TPU:4 before, /device:TPU:30 now
where the time goes in v1:
time: 59.8 us; the launch traced here: 59.5 us
  Pallas kernels  52 us (87%)
  local copies, waits for them, and re-layouts  7.46 us (12%)
    pallas_call x1, Pallas kernels, shards(): pl.pallas_call(kernel, out_shape=jax.ShapeDtypeStruct((NC, CH, ROWS), BF1...  52 us
    unnamed x13, local copies, waits for them, and re-layouts  6.78 us

profile of v1, /device:TPU:30, one launch (start us, length us, event | category | flops | bytes accessed | tf_op | source)
XLA Modules:
  0.0 59.5 jit_solution(12098287053410868838)
XLA Ops:
  0.0 0.7 %reshape.18.gain_ref = bf16[1,1024]{1,0:T(2,128)(2,1)S(1)} reshape(bf16[1024]{0:T(1024)(128)(2,1)} %param.13) | data formatting | bytes 4096 | tf_op jit(solution)/shard_map/reshape | solution.py:387
  0.7 0.0 copy-start
  0.7 1.4 %copy-done = bf16[768,1024]{1,0:T(8,128)(2,1)S(1)} copy-done((bf16[768,1024]{1,0:T(8,128)(2,1)S(1)}, bf16[768,1024]{1,0:T(8,128)(2,1)}, u32[]{:S(2)}) %copy-start) | copy-done | bytes 1572888
  2.1 0.0 copy-start.1
  2.1 0.9 %copy-done.1 = bf16[768,128]{1,0:T(8,128)(2,1)S(1)} copy-done((bf16[768,128]{1,0:T(8,128)(2,1)S(1)}, bf16[768,128]{1,0:T(8,128)(2,1)}, u32[]{:S(2)}) %copy-start.1) | copy-done | bytes 196632
  3.0 0.0 copy-start.2
  3.0 0.9 %copy-done.2 = bf16[768,128]{1,0:T(8,128)(2,1)S(1)} copy-done((bf16[768,128]{1,0:T(8,128)(2,1)S(1)}, bf16[768,128]{1,0:T(8,128)(2,1)}, u32[]{:S(2)}) %copy-start.2) | copy-done | bytes 196632
  3.9 0.0 copy-start.3
  4.0 0.9 %copy-done.3 = bf16[7,16,768]{2,1,0:T(8,128)(2,1)S(1)} copy-done((bf16[7,16,768]{2,1,0:T(8,128)(2,1)S(1)}, bf16[7,16,768]{2,1,0:T(8,128)(2,1)}, u32[]{:S(2)}) %copy-start.3) | copy-done | bytes 172056
  4.9 0.0 copy-start.4
  4.9 0.8 %copy-done.4 = f32[16,768]{1,0:T(8,128)S(1)} copy-done((f32[16,768]{1,0:T(8,128)S(1)}, f32[16,768]{1,0:T(8,128)}, u32[]{:S(2)}) %copy-start.4) | copy-done | bytes 49176
  5.7 0.0 copy-start.5
  5.7 0.7 %copy-done.5 = f32[16]{0:T(128)S(1)} copy-done((f32[16]{0:T(128)S(1)}, f32[16]{0:T(128)}, u32[]{:S(2)}) %copy-start.5) | copy-done | bytes 88
  6.3 52.0 %layer.1 = bf16[6,128,1024]{2,1,0:T(8,128)(2,1)S(1)} custom-call(bf16[6,128,128]{2,1,0:T(8,128)(2,1)S(1)} %bitcast.6, bf16[6,128,128]{2,1,0:T(8,128)(2,1)S(1)} %bitcast.7, bf16[6,128,1024]{2,1,0:T(8,128)(2,1)S(1)} %bitcast.5, f32[16,768]{1,0:T(8,128)S(1)} %copy-done.4, bf16[7,16,768]{2,1,0:T(8,128)(2,1)S(1)} %copy-done.3, f32[16]{0:T(128)S(1)} %copy-done.5, ...), custom_call_target="tpu_custom_call" | custom-call | tf_op jit(solution)/shard_map/layer/pallas_call | solution.py:354
  58.4 1.1 %copy.9 = bf16[768,1024]{1,0:T(8,128)(2,1)} copy(bf16[768,1024]{1,0:T(8,128)(2,1)S(1)} %bitcast.4) | data formatting | bytes 3145728
Async XLA Ops:
  0.7 1.4 %copy-start = (bf16[768,1024]{1,0:T(8,128)(2,1)S(1)}, bf16[768,1024]{1,0:T(8,128)(2,1)}, u32[]{:S(2)}) copy-start(bf16[768,1024]{1,0:T(8,128)(2,1)} %param.9) | copy-start | bytes 4718596
  2.1 0.9 %copy-start.1 = (bf16[768,128]{1,0:T(8,128)(2,1)S(1)}, bf16[768,128]{1,0:T(8,128)(2,1)}, u32[]{:S(2)}) copy-start(bf16[768,128]{1,0:T(8,128)(2,1)} %param.7) | copy-start | bytes 589828
  3.0 0.9 %copy-start.2 = (bf16[768,128]{1,0:T(8,128)(2,1)S(1)}, bf16[768,128]{1,0:T(8,128)(2,1)}, u32[]{:S(2)}) copy-start(bf16[768,128]{1,0:T(8,128)(2,1)} %param.8) | copy-start | bytes 589828
  3.9 0.9 %copy-start.3 = (bf16[7,16,768]{2,1,0:T(8,128)(2,1)S(1)}, bf16[7,16,768]{2,1,0:T(8,128)(2,1)}, u32[]{:S(2)}) copy-start(bf16[7,16,768]{2,1,0:T(8,128)(2,1)} %lw_ref.1) | copy-start | bytes 516100
  4.9 0.8 %copy-start.4 = (f32[16,768]{1,0:T(8,128)S(1)}, f32[16,768]{1,0:T(8,128)}, u32[]{:S(2)}) copy-start(f32[16,768]{1,0:T(8,128)} %ld_ref.1) | copy-start | bytes 147460
  5.7 0.7 %copy-start.5 = (f32[16]{0:T(128)S(1)}, f32[16]{0:T(128)}, u32[]{:S(2)}) copy-start(f32[16]{0:T(128)} %skip_ref.1) | copy-start | bytes 196

commit v2 on v1

v2 whole, which is shorter than its diff:
```python
import jax
import jax.numpy as jnp
from jax import lax
from jax.experimental import pallas as pl
from jax.experimental.pallas import tpu as pltpu
from jax.sharding import PartitionSpec as P

F32 = jnp.float32
BF16 = jnp.bfloat16
NT = (((1,), (1,)), ((), ()))

TOK = 768
CH = 128
NC = TOK // CH
HEADS = 16
HH = HEADS // 2
DIM = 64
STATE = 128
ROWS = HEADS * DIM
HALF = ROWS // 2
PLANE = 32
CHIPS = 16
SLICE = HALF // CHIPS
LEVELS = 6
GROUP = 8
CHANNELS = 8192
STARTS = {2: 0, 3: 4, 4: 6, 5: 7}


def rows_of(start, size):
    return pl.ds(pl.multiple_of(start, SLICE), size)


def kernel(
    q_hbm, k_hbm, v_hbm, ld_hbm, lw_hbm, skip_hbm, gain_hbm, out_ref,
    q_ref, k_ref, v_ref, ld_ref, lw_ref, skip_ref, gain_ref, in_sem,
    lc_ref, lct_ref, w0_ref, ci_ref, cum_ref, coef_ref, vt_ref, rb_ref, st_ref, acc_ref, y_ref,
    comb_ref, pcomb_ref, fall_ref, pair_ref, crow_ref, crows_ref,
    gath_ref, node_ref, bucket_ref, zin_ref, bb_ref, sq_ref, sqs_ref,
    ex_ss, ex_rs, cb_ss, cb_rs, l0_ss, l0_rs, cr_ss, cr_rs, p1_ss, p1_rs, n1_ss, n1_rs,
    p2_ss, p2_rs, z_ss, z_rs, fw_ss, fw_rs, sq_ss, sq_rs,
):
    seq = lax.axis_index("seq")
    head = lax.axis_index("head")
    zhi = seq // PLANE
    me = seq % PLANE
    chip = me // 2
    core = me % 2
    base = zhi * PLANE
    bits = [core] + [(chip // (1 << b)) % 2 for b in range(4)] + [zhi]

    def at(s):
        return {"seq": s, "head": head}

    def same_core(to):
        return at(base + 2 * to + core)

    def remote(src, dst, ss, rs, device):
        return pltpu.make_async_remote_copy(
            src_ref=src, dst_ref=dst, send_sem=ss, recv_sem=rs,
            device_id=device, device_id_type=pl.DeviceIdType.MESH,
        )

    partner = at(base + me + 1 - 2 * core)
    zpeer = at(seq + PLANE - 2 * PLANE * zhi)
    half = rows_of(HALF * core, HALF)
    other = rows_of(HALF * (1 - core), HALF)
    mine = HALF * core + SLICE * chip

    pairs = [(ld_hbm, ld_ref), (k_hbm, k_ref), (lw_hbm, lw_ref), (q_hbm, q_ref),
             (skip_hbm, skip_ref), (gain_hbm, gain_ref)]
    loads = [pltpu.make_async_copy(src, dst, in_sem.at[i]) for i, (src, dst) in enumerate(pairs)]
    loads[0].start()
    for c in range(NC):
        pltpu.make_async_copy(v_hbm.at[c], v_ref.at[c], in_sem.at[6 + c]).start()
    for copy in loads[1:]:
        copy.start()

    barrier = pltpu.get_barrier_semaphore()

    def greet(device):
        pl.semaphore_signal(
            barrier, inc=1, device_id=device, device_id_type=pl.DeviceIdType.MESH)

    @pl.loop(1, CHIPS)
    def _(r):
        greet(same_core((chip + r) % CHIPS))

    @pl.loop(1, GROUP)
    def _(r):
        greet({"seq": seq, "head": (head + r) % GROUP})

    greet(partner)

    @pl.when(zhi == 1)
    def _():
        greet(zpeer)

    loads[0].wait()
    loads[2].wait()
    row = lax.broadcasted_iota(jnp.int32, (CH, CH), 0)
    col = lax.broadcasted_iota(jnp.int32, (CH, CH), 1)
    tri = jnp.where(row <= col, 1.0, 0.0).astype(BF16)
    his, mids, los = [], [], []
    for c in range(NC):
        x = ld_ref[:, c * CH:(c + 1) * CH]
        hi = x.astype(BF16)
        rest = x - hi.astype(F32)
        mid = rest.astype(BF16)
        his.append(hi)
        mids.append(mid)
        los.append((rest - mid.astype(F32)).astype(BF16))
    sums = jnp.dot(jnp.concatenate(his + mids + los, axis=0), tri, preferred_element_type=F32)
    n = HEADS * NC
    total = jnp.zeros((HEADS, CH), F32)
    trow = jnp.zeros((1, CH), F32)
    for c in range(NC):
        a = HEADS * c
        lc = sums[a:a + HEADS] + sums[n + a:n + a + HEADS] + sums[2 * n + a:2 * n + a + HEADS]
        lc_ref[c] = lc
        cum_ref[c] = lc + total
        turned = jnp.concatenate([lc, jnp.zeros((CH - HEADS, CH), F32)], axis=0).T
        lct_ref[c] = turned
        trow = trow + turned[CH - 1:CH]
        w0 = lw_ref[0, :, c * CH:(c + 1) * CH].astype(F32)
        w0_ref[c] = w0
        ci_ref[c] = w0 * jnp.exp(lc)
        total = total + jnp.broadcast_to(lc[:, CH - 1:CH], (HEADS, CH))
    comb_ref[0:HEADS] = total
    comb_ref[HEADS:HEADS + 8] = jnp.broadcast_to(trow, (8, CH))

    st_ref[...] = jnp.zeros((ROWS, STATE), F32)
    loads[1].wait()

    @pl.loop(0, NC)
    def _(c):
        pltpu.make_async_copy(v_hbm.at[c], v_ref.at[c], in_sem.at[6 + c]).wait()
        lc = lc_ref[c]
        last = jnp.broadcast_to(lc[:, CH - 1:CH], (HEADS, CH))
        fall = jnp.exp(last)
        tail = jnp.exp(last - lc)
        scaled = []
        for j in range(ROWS // CH):
            vt = v_ref[c, :, j * CH:(j + 1) * CH].T
            vt_ref[c, j * CH:(j + 1) * CH, :] = vt
            wide = vt.astype(F32)
            for i in range(2):
                h = 2 * j + i
                scaled.append((wide[i * DIM:(i + 1) * DIM] * tail[h:h + 1]).astype(BF16))
        new = jnp.dot(jnp.concatenate(scaled, axis=0), k_ref[c], preferred_element_type=F32)
        for h in range(HEADS):
            rows = slice(h * DIM, (h + 1) * DIM)
            old = st_ref[rows]
            rb_ref[c, rows] = old.astype(BF16)
            st_ref[rows] = fall[h:h + 1] * old + new[rows]

    pl.semaphore_wait(barrier, CHIPS - 1 + GROUP - 1 + 1 + 1 - zhi)

    swap = remote(st_ref.at[other], bucket_ref.at[0, other], ex_ss, ex_rs, partner)
    comb = remote(comb_ref, pcomb_ref, cb_ss, cb_rs, partner)
    zero = remote(st_ref.at[half], bucket_ref.at[0, half], l0_ss, l0_rs, partner)
    swap.start()
    comb.start()

    @pl.when(core == 0)
    def _():
        zero.start()

    for copy in loads[3:]:
        copy.wait()

    def inside(first, last):
        @pl.loop(first, last)
        def _(c):
            qc = q_ref[c]
            s = lax.dot_general(k_ref[c], qc, NT, preferred_element_type=F32)
            r0 = lax.broadcasted_iota(jnp.int32, (CH, CH), 0)
            c0 = lax.broadcasted_iota(jnp.int32, (CH, CH), 1)
            s = jnp.where(r0 <= c0, s, 0.0)
            inter = lax.dot_general(rb_ref[c], qc, NT, preferred_element_type=F32)
            for h in range(HEADS):
                rows = slice(h * DIM, (h + 1) * DIM)
                d = jnp.minimum(lc_ref[c, h:h + 1] - lct_ref[c, :, h:h + 1], 0.0)
                mix = (jnp.exp(d) * s).astype(BF16)
                vt = vt_ref[c, rows]
                o = jnp.dot(vt, mix, preferred_element_type=F32)
                acc_ref[c, rows] = (
                    w0_ref[c, h:h + 1] * o + ci_ref[c, h:h + 1] * inter[rows]
                    + skip_ref[h] * vt.astype(F32))

    inside(0, 2)

    comb.wait_recv()
    remote(st_ref.at[half], bucket_ref.at[0, half], ex_ss, ex_rs, partner).wait_recv()
    late = jnp.where(core == 0, pcomb_ref[0:HEADS], comb_ref[0:HEADS])
    fall_ref[...] = jnp.exp(late)
    for i in range(HH):
        at_head = rows_of(HALF * core + DIM * i, DIM)
        own, got = st_ref[at_head], bucket_ref[0, at_head]
        left = jnp.where(core == 0, own, got)
        right = jnp.where(core == 0, got, own)
        pair_ref[i * DIM:(i + 1) * DIM] = fall_ref[pl.ds(HH * core + i, 1), :] * left + right
    crow = comb_ref[HEADS:HEADS + 1] + pcomb_ref[HEADS:HEADS + 1]
    crow_ref[...] = crow
    crows_ref[chip] = crow

    @pl.loop(1, CHIPS)
    def _(r):
        to = (chip + r) % CHIPS
        remote(pair_ref.at[rows_of(SLICE * to, SLICE)], gath_ref.at[chip], p1_ss, p1_rs,
               same_core(to)).start()
        remote(crow_ref, crows_ref.at[chip], cr_ss, cr_rs, same_core(to)).start()

    first_level = remote(
        pair_ref, bucket_ref.at[1, half], n1_ss, n1_rs, same_core(chip + 1 - 2 * bits[1]))

    @pl.when(bits[1] == 0)
    def _():
        first_level.start()

    gath_ref[chip] = pair_ref[rows_of(SLICE * chip, SLICE)]

    inside(2, NC)

    fifteen = pl.ds(0, CHIPS - 1)
    crs = remote(crows_ref.at[fifteen], crows_ref.at[fifteen], cr_ss, cr_rs, partner)
    p1s = remote(gath_ref.at[fifteen], gath_ref.at[fifteen], p1_ss, p1_rs, partner)
    crs.wait_recv()
    p1s.wait_recv()

    lane = lax.broadcasted_iota(jnp.int32, (1, CH), 1)
    pick = lane == HH * core + chip // 2
    nodes = [gath_ref[i] for i in range(CHIPS)]
    weights = [
        jnp.sum(jnp.where(pick, crows_ref[i], 0.0), axis=1, keepdims=True) for i in range(CHIPS)]
    slot = 0
    for level in range(2, LEVELS):
        count = len(nodes) // 2
        joined = [
            jnp.exp(jnp.broadcast_to(weights[2 * j + 1], (1, CH))) * nodes[2 * j] + nodes[2 * j + 1]
            for j in range(count)
        ]
        weights = [weights[2 * j] + weights[2 * j + 1] for j in range(count)]
        nodes = joined
        for j in range(0, count, 2):
            node_ref[slot] = nodes[j]
            slot += 1

    up = remote(node_ref.at[STARTS[5]], zin_ref, z_ss, z_rs, zpeer)

    @pl.when(zhi == 0)
    def _():
        up.start()

    @pl.loop(1, CHIPS)
    def _(r):
        to = (chip + r) % CHIPS
        for level in range(2, 5):
            @pl.when((to // (1 << (level - 1))) % 2 == 1)
            def _():
                remote(
                    node_ref.at[STARTS[level] + to // (1 << level)],
                    bucket_ref.at[level, rows_of(mine, SLICE)],
                    p2_ss.at[level], p2_rs.at[level], same_core(to)).start()

    for level in range(2, 5):
        @pl.when(bits[level] == 1)
        def _():
            bucket_ref[level, rows_of(mine, SLICE)] = node_ref[STARTS[level] + chip // (1 << level)]

    before = [jnp.zeros((1, CH), F32) for _ in range(LEVELS)]
    for i in range(CHIPS - 1):
        t = crows_ref[i]
        for level in range(2, LEVELS):
            counts = (i < chip) & (i >= chip - chip % (1 << (level - 1)))
            before[level] = before[level] + jnp.where(counts, t, 0.0)
    turned = jnp.concatenate(before + [jnp.zeros((CH - LEVELS, CH), F32)], axis=0).T
    inner = jnp.where(core == 1, pcomb_ref[0:HEADS], 0.0)
    for level in range(LEVELS):
        off = jnp.zeros((HEADS, CH), F32)
        if level > 0:
            off = inner
        if level > 1:
            off = off + jnp.broadcast_to(turned[0:HEADS, level:level + 1], (HEADS, CH))
        for c in range(NC):
            w = lw_ref[level + 1, :, c * CH:(c + 1) * CH].astype(F32)
            coef_ref[level, c] = w * jnp.exp(cum_ref[c] + off)

    def cross(level, side):
        at_half = rows_of(HALF * side, HALF)
        bb_ref[...] = bucket_ref[level, at_half].astype(BF16)

        @pl.loop(0, NC // 2)
        def _(d):
            q2 = q_ref[pl.ds(2 * d, 2)].reshape(2 * CH, STATE)
            o = lax.dot_general(bb_ref[...], q2, NT, preferred_element_type=F32)
            for i in range(2):
                c = 2 * d + i
                for h in range(HH):
                    rows = rows_of(HALF * side + DIM * h, DIM)
                    acc_ref[c, rows] = (
                        acc_ref[c, rows]
                        + coef_ref[level, c, pl.ds(HH * side + h, 1), :]
                        * o[h * DIM:(h + 1) * DIM, i * CH:(i + 1) * CH])

    def forward(level):
        return remote(
            bucket_ref.at[level, half], bucket_ref.at[level, half],
            fw_ss.at[level], fw_rs.at[level], partner)

    def forwarded(level):
        return remote(
            bucket_ref.at[level, other], bucket_ref.at[level, other],
            fw_ss.at[level], fw_rs.at[level], partner)

    some = pl.ds(0, (CHIPS - 1) * SLICE)

    def slices(level):
        part = bucket_ref.at[level, some]
        return remote(part, part, p2_ss.at[level], p2_rs.at[level], partner)

    @pl.when(core == 1)
    def _():
        cross(0, core)
        remote(st_ref.at[other], bucket_ref.at[0, other], l0_ss, l0_rs, partner).wait_recv()
        cross(0, 1 - core)

    @pl.when(bits[1] == 1)
    def _():
        first_level.wait_recv()
        forward(1).start()
        cross(1, core)
        forwarded(1).wait_recv()
        cross(1, 1 - core)

    @pl.when(zhi == 1)
    def _():
        up.wait_recv()

        @pl.loop(1, CHIPS)
        def _(r):
            remote(
                zin_ref, bucket_ref.at[5, rows_of(mine, SLICE)],
                p2_ss.at[5], p2_rs.at[5], same_core((chip + r) % CHIPS)).start()
        bucket_ref[5, rows_of(mine, SLICE)] = zin_ref[...]

    for level in range(2, 5):
        @pl.when(bits[level] == 1)
        def _():
            slices(level).wait_recv()
            forward(level).start()

    for level in range(2, 5):
        @pl.when(bits[level] == 1)
        def _():
            cross(level, core)
            forwarded(level).wait_recv()
            cross(level, 1 - core)

    @pl.when(zhi == 1)
    def _():
        slices(5).wait_recv()
        forward(5).start()

    @pl.when(zhi == 1)
    def _():
        cross(5, core)
        forwarded(5).wait_recv()
        cross(5, 1 - core)

    sq_ref[...] = jnp.zeros((8, CH), F32)
    for c in range(NC):
        y = acc_ref[c]
        sq_ref[c:c + 1] = jnp.sum(y * y, axis=0, keepdims=True)
    sqs_ref[head] = sq_ref[...]

    @pl.loop(1, GROUP)
    def _(r):
        remote(
            sq_ref, sqs_ref.at[head], sq_ss, sq_rs,
            {"seq": seq, "head": (head + r) % GROUP}).start()

    gain = gain_ref[...].reshape(1, ROWS).astype(F32)

    @pl.loop(0, NC)
    def _(c):
        for j in range(ROWS // CH):
            cols = slice(j * CH, (j + 1) * CH)
            y_ref[c, :, cols] = acc_ref[c, cols].T * gain[:, cols]

    swap.wait_send()
    comb.wait_send()
    crs.wait_send()
    p1s.wait_send()

    @pl.when(core == 0)
    def _():
        zero.wait_send()

    @pl.when(bits[1] == 0)
    def _():
        first_level.wait_send()

    @pl.when(bits[1] == 1)
    def _():
        forward(1).wait_send()

    for level in range(2, 5):
        for has in range(2):
            @pl.when(bits[level] == has)
            def _():
                sent = bucket_ref.at[level, pl.ds(0, (CHIPS // 2 - has) * SLICE)]
                remote(sent, sent, p2_ss.at[level], p2_rs.at[level], partner).wait_send()

        @pl.when(bits[level] == 1)
        def _():
            forward(level).wait_send()

    @pl.when(zhi == 0)
    def _():
        up.wait_send()

    @pl.when(zhi == 1)
    def _():
        slices(5).wait_send()
        forward(5).wait_send()

    seven = sqs_ref.at[pl.ds(0, GROUP - 1)]
    remote(seven, seven, sq_ss, sq_rs, partner).wait_recv()
    remote(seven, seven, sq_ss, sq_rs, partner).wait_send()

    whole = sqs_ref[0]
    for g in range(1, GROUP):
        whole = whole + sqs_ref[g]
    inv = lax.rsqrt(whole / CHANNELS + 1e-05)
    turned = jnp.concatenate([inv, jnp.zeros((CH - 8, CH), F32)], axis=0).T
    for c in range(NC):
        out_ref[c] = (y_ref[c] * turned[:, c:c + 1]).astype(BF16)


def shards(queries, keys, values, log_decay, level_weight, skip, norm_gain):
    hbm = pl.BlockSpec(memory_space=pltpu.HBM)
    dma = pltpu.SemaphoreType.DMA

    def stay(x):
        return pltpu.with_memory_space_constraint(x, pltpu.HBM)

    out = pl.pallas_call(
        kernel,
        out_shape=jax.ShapeDtypeStruct((NC, CH, ROWS), BF16),
        in_specs=[hbm] * 7,
        out_specs=pl.BlockSpec(memory_space=pltpu.VMEM),
        scratch_shapes=[
            pltpu.VMEM((NC, CH, STATE), BF16),
            pltpu.VMEM((NC, CH, STATE), BF16),
            pltpu.VMEM((NC, CH, ROWS), BF16),
            pltpu.VMEM((HEADS, TOK), F32),
            pltpu.VMEM((LEVELS + 1, HEADS, TOK), BF16),
            pltpu.SMEM((HEADS,), F32),
            pltpu.VMEM((ROWS,), BF16),
            dma((6 + NC,)),
            pltpu.VMEM((NC, HEADS, CH), F32),
            pltpu.VMEM((NC, CH, CH), F32),
            pltpu.VMEM((NC, HEADS, CH), F32),
            pltpu.VMEM((NC, HEADS, CH), F32),
            pltpu.VMEM((NC, HEADS, CH), F32),
            pltpu.VMEM((LEVELS, NC, HEADS, CH), F32),
            pltpu.VMEM((NC, ROWS, CH), BF16),
            pltpu.VMEM((NC, ROWS, STATE), BF16),
            pltpu.VMEM((ROWS, STATE), F32),
            pltpu.VMEM((NC, ROWS, CH), F32),
            pltpu.VMEM((NC, CH, ROWS), F32),
            pltpu.VMEM((HEADS + 8, CH), F32),
            pltpu.VMEM((HEADS + 8, CH), F32),
            pltpu.VMEM((HEADS, CH), F32),
            pltpu.VMEM((HALF, STATE), F32),
            pltpu.VMEM((1, CH), F32),
            pltpu.VMEM((CHIPS, 1, CH), F32),
            pltpu.VMEM((CHIPS, SLICE, STATE), F32),
            pltpu.VMEM((8, SLICE, STATE), F32),
            pltpu.VMEM((LEVELS, ROWS, STATE), F32),
            pltpu.VMEM((SLICE, STATE), F32),
            pltpu.VMEM((HALF, STATE), BF16),
            pltpu.VMEM((8, CH), F32),
            pltpu.VMEM((GROUP, 8, CH), F32),
            dma, dma, dma, dma, dma, dma, dma, dma, dma, dma, dma, dma,
            dma((LEVELS,)), dma((LEVELS,)), dma, dma, dma((LEVELS,)), dma((LEVELS,)), dma, dma,
        ],
        compiler_params=pltpu.CompilerParams(
            collective_id=0, has_side_effects=True, vmem_limit_bytes=50 << 20),
        name="layer",
    )(
        stay(queries.reshape(NC, CH, STATE)), stay(keys.reshape(NC, CH, STATE)),
        stay(values.reshape(NC, CH, ROWS)), stay(log_decay), stay(level_weight), stay(skip),
        stay(norm_gain),
    )
    return out.reshape(TOK, ROWS)


def solution(mesh):
    placed = (
        P("seq", None), P("seq", None), P("seq", "head"), P("head", "seq"),
        P(None, "head", "seq"), P("head"), P("head"),
    )
    return jax.shard_map(
        shards, mesh=mesh, in_specs=placed, out_specs=P("seq", "head"), check_vma=False
    )
```

time: 59.8 us -> 45.9 us (0.77)
  Pallas kernels: 52 us -> 44.6 us
  local copies, waits for them, and re-layouts: 7.46 us -> 1.15 us
    pallas_call x1, Pallas kernels: 52 us -> 44.6 us  [shards(): pl.pallas_call(kernel, out_shape=jax.ShapeDtypeStruct((NC, CH, ROWS), BF1...]
    unnamed x13 -> x1, local copies, waits for them, and re-layouts: 6.78 us -> 1.15 us
    reshape x1 -> x0, local copies, waits for them, and re-layouts: 0.69 us -> none  [shards(): norm_gain.reshape(1, ROWS)]
where the time goes in v2:
time: 45.9 us; the launch traced here: 45.7 us
  Pallas kernels  44.6 us (97%)
  local copies, waits for them, and re-layouts  1.15 us (3%)
    pallas_call x1, Pallas kernels, shards(): pl.pallas_call(kernel, out_shape=jax.ShapeDtypeStruct((NC, CH, ROWS), BF1...  44.6 us
    unnamed x1, local copies, waits for them, and re-layouts  1.15 us

profile of v2, /device:TPU:30, one launch (start us, length us, event | category | flops | bytes accessed | tf_op | source)
XLA Modules:
  0.0 45.7 jit_solution(18105848666031796205)
XLA Ops:
  0.0 44.6 %layer.1 = bf16[6,128,1024]{2,1,0:T(8,128)(2,1)S(1)} custom-call(bf16[6,128,128]{2,1,0:T(8,128)(2,1)} %bitcast.6, bf16[6,128,128]{2,1,0:T(8,128)(2,1)} %bitcast.7, bf16[6,128,1024]{2,1,0:T(8,128)(2,1)} %bitcast.5, f32[16,768]{1,0:T(8,128)} %ld_hbm.1, bf16[7,16,768]{2,1,0:T(8,128)(2,1)} %lw_hbm.1, f32[16]{0:T(128)} %skip_hbm.1, bf16[1024]{0:T(1024)(128)(2,1)} %gain_hbm.1), custom_call_target="tpu_custom_call" | custom-call | tf_op jit(solution)/shard_map/layer/pallas_call | solution.py:448
  44.6 1.1 %copy.9 = bf16[768,1024]{1,0:T(8,128)(2,1)} copy(bf16[768,1024]{1,0:T(8,128)(2,1)S(1)} %bitcast.4) | data formatting | bytes 3145728

commit v3 on v2

--- a/solution.py
+++ b/solution.py
@@ -36,9 +36,9 @@
     q_ref, k_ref, v_ref, ld_ref, lw_ref, skip_ref, gain_ref, in_sem,
     lc_ref, lct_ref, w0_ref, ci_ref, cum_ref, coef_ref, vt_ref, rb_ref, st_ref, acc_ref, y_ref,
     comb_ref, pcomb_ref, fall_ref, pair_ref, crow_ref, crows_ref,
-    gath_ref, node_ref, bucket_ref, zin_ref, bb_ref, sq_ref, sqs_ref,
+    gath_ref, node_ref, bucket_ref, qt_ref, bb_ref, sq_ref, sqs_ref,
     ex_ss, ex_rs, cb_ss, cb_rs, l0_ss, l0_rs, cr_ss, cr_rs, p1_ss, p1_rs, n1_ss, n1_rs,
-    p2_ss, p2_rs, z_ss, z_rs, fw_ss, fw_rs, sq_ss, sq_rs,
+    p2_ss, p2_rs, z_ss, z_rs, fw_ss, fw_rs, sq_ss, sq_rs, here_z, here_h,
 ):
     seq = lax.axis_index("seq")
     head = lax.axis_index("head")
@@ -78,26 +78,34 @@
 
     barrier = pltpu.get_barrier_semaphore()
 
-    def greet(device):
-        pl.semaphore_signal(
-            barrier, inc=1, device_id=device, device_id_type=pl.DeviceIdType.MESH)
+    def greet(device, sem=barrier):
+        pl.semaphore_signal(sem, inc=1, device_id=device, device_id_type=pl.DeviceIdType.MESH)
+
+    def rank_of(h):
+        return h + zhi * (GROUP - 1 - 2 * h)
+
+    def peer(r):
+        return (head + r) % GROUP
+
+    rank = rank_of(head)
 
     @pl.loop(1, CHIPS)
     def _(r):
         greet(same_core((chip + r) % CHIPS))
 
+    greet(partner)
+
+    @pl.when(zhi == 0)
+    def _():
+        greet(zpeer)
+
     @pl.loop(1, GROUP)
     def _(r):
-        greet({"seq": seq, "head": (head + r) % GROUP})
-
-    greet(partner)
-
-    @pl.when(zhi == 1)
-    def _():
-        greet(zpeer)
+        @pl.when(rank_of(peer(r)) > rank)
+        def _():
+            greet({"seq": seq, "head": peer(r)})
 
     loads[0].wait()
-    loads[2].wait()
     row = lax.broadcasted_iota(jnp.int32, (CH, CH), 0)
     col = lax.broadcasted_iota(jnp.int32, (CH, CH), 1)
     tri = jnp.where(row <= col, 1.0, 0.0).astype(BF16)
@@ -122,9 +130,6 @@
         turned = jnp.concatenate([lc, jnp.zeros((CH - HEADS, CH), F32)], axis=0).T
         lct_ref[c] = turned
         trow = trow + turned[CH - 1:CH]
-        w0 = lw_ref[0, :, c * CH:(c + 1) * CH].astype(F32)
-        w0_ref[c] = w0
-        ci_ref[c] = w0 * jnp.exp(lc)
         total = total + jnp.broadcast_to(lc[:, CH - 1:CH], (HEADS, CH))
     comb_ref[0:HEADS] = total
     comb_ref[HEADS:HEADS + 8] = jnp.broadcast_to(trow, (8, CH))
@@ -154,7 +159,7 @@
             rb_ref[c, rows] = old.astype(BF16)
             st_ref[rows] = fall[h:h + 1] * old + new[rows]
 
-    pl.semaphore_wait(barrier, CHIPS - 1 + GROUP - 1 + 1 + 1 - zhi)
+    pl.semaphore_wait(barrier, CHIPS - 1 + 1 + rank + zhi)
 
     swap = remote(st_ref.at[other], bucket_ref.at[0, other], ex_ss, ex_rs, partner)
     comb = remote(comb_ref, pcomb_ref, cb_ss, cb_rs, partner)
@@ -162,12 +167,24 @@
     swap.start()
     comb.start()
 
-    @pl.when(core == 0)
-    def _():
-        zero.start()
-
+    @pl.when(zhi == 1)
+    def _():
+        greet(zpeer, here_z)
+
+    @pl.loop(1, GROUP)
+    def _(r):
+        @pl.when(rank_of(peer(r)) < rank)
+        def _():
+            greet({"seq": seq, "head": peer(r)}, here_h)
+
+    loads[2].wait()
     for copy in loads[3:]:
         copy.wait()
+    for c in range(NC):
+        w0 = lw_ref[0, :, c * CH:(c + 1) * CH].astype(F32)
+        w0_ref[c] = w0
+        ci_ref[c] = w0 * jnp.exp(lc_ref[c])
+        qt_ref[c // 2, :, (c % 2) * CH:(c % 2 + 1) * CH] = q_ref[c].T
 
     def inside(first, last):
         @pl.loop(first, last)
@@ -211,6 +228,10 @@
                same_core(to)).start()
         remote(crow_ref, crows_ref.at[chip], cr_ss, cr_rs, same_core(to)).start()
 
+    @pl.when(core == 0)
+    def _():
+        zero.start()
+
     first_level = remote(
         pair_ref, bucket_ref.at[1, half], n1_ss, n1_rs, same_core(chip + 1 - 2 * bits[1]))
 
@@ -246,22 +267,25 @@
             node_ref[slot] = nodes[j]
             slot += 1
 
-    up = remote(node_ref.at[STARTS[5]], zin_ref, z_ss, z_rs, zpeer)
-
-    @pl.when(zhi == 0)
-    def _():
-        up.start()
-
-    @pl.loop(1, CHIPS)
-    def _(r):
-        to = (chip + r) % CHIPS
-        for level in range(2, 5):
+    up = remote(
+        node_ref.at[STARTS[5]], bucket_ref.at[5, rows_of(mine, SLICE)], z_ss, z_rs, zpeer)
+
+    for level in range(2, 5):
+        @pl.loop(1, CHIPS)
+        def _(r):
+            to = (chip + r) % CHIPS
+
             @pl.when((to // (1 << (level - 1))) % 2 == 1)
             def _():
                 remote(
                     node_ref.at[STARTS[level] + to // (1 << level)],
                     bucket_ref.at[level, rows_of(mine, SLICE)],
                     p2_ss.at[level], p2_rs.at[level], same_core(to)).start()
+
+    @pl.when(zhi == 0)
+    def _():
+        pl.semaphore_wait(here_z, 1)
+        up.start()
 
     for level in range(2, 5):
         @pl.when(bits[level] == 1)
@@ -290,10 +314,8 @@
         at_half = rows_of(HALF * side, HALF)
         bb_ref[...] = bucket_ref[level, at_half].astype(BF16)
 
-        @pl.loop(0, NC // 2)
-        def _(d):
-            q2 = q_ref[pl.ds(2 * d, 2)].reshape(2 * CH, STATE)
-            o = lax.dot_general(bb_ref[...], q2, NT, preferred_element_type=F32)
+        for d in range(NC // 2):
+            o = jnp.dot(bb_ref[...], qt_ref[d], preferred_element_type=F32)
             for i in range(2):
                 c = 2 * d + i
                 for h in range(HH):
@@ -325,6 +347,15 @@
         remote(st_ref.at[other], bucket_ref.at[0, other], l0_ss, l0_rs, partner).wait_recv()
         cross(0, 1 - core)
 
+    @pl.when(zhi == 1)
+    def _():
+        up.wait_recv()
+        own = bucket_ref.at[5, rows_of(mine, SLICE)]
+
+        @pl.loop(1, CHIPS)
+        def _(r):
+            remote(own, own, p2_ss.at[5], p2_rs.at[5], same_core((chip + r) % CHIPS)).start()
+
     @pl.when(bits[1] == 1)
     def _():
         first_level.wait_recv()
@@ -333,46 +364,39 @@
         forwarded(1).wait_recv()
         cross(1, 1 - core)
 
-    @pl.when(zhi == 1)
-    def _():
-        up.wait_recv()
-
-        @pl.loop(1, CHIPS)
-        def _(r):
-            remote(
-                zin_ref, bucket_ref.at[5, rows_of(mine, SLICE)],
-                p2_ss.at[5], p2_rs.at[5], same_core((chip + r) % CHIPS)).start()
-        bucket_ref[5, rows_of(mine, SLICE)] = zin_ref[...]
-
     for level in range(2, 5):
         @pl.when(bits[level] == 1)
         def _():
             slices(level).wait_recv()
             forward(level).start()
-
-    for level in range(2, 5):
+            cross(level, core)
+
+    def rest(level):
         @pl.when(bits[level] == 1)
         def _():
-            cross(level, core)
             forwarded(level).wait_recv()
             cross(level, 1 - core)
 
+    rest(2)
+
     @pl.when(zhi == 1)
     def _():
         slices(5).wait_recv()
         forward(5).start()
-
-    @pl.when(zhi == 1)
-    def _():
         cross(5, core)
-        forwarded(5).wait_recv()
-        cross(5, 1 - core)
+
+    for level in range(3, LEVELS):
+        rest(level)
 
     sq_ref[...] = jnp.zeros((8, CH), F32)
     for c in range(NC):
         y = acc_ref[c]
         sq_ref[c:c + 1] = jnp.sum(y * y, axis=0, keepdims=True)
     sqs_ref[head] = sq_ref[...]
+
+    @pl.when(rank < GROUP - 1)
+    def _():
+        pl.semaphore_wait(here_h, GROUP - 1 - rank)
 
     @pl.loop(1, GROUP)
     def _(r):
@@ -479,12 +503,13 @@
             pltpu.VMEM((CHIPS, SLICE, STATE), F32),
             pltpu.VMEM((8, SLICE, STATE), F32),
             pltpu.VMEM((LEVELS, ROWS, STATE), F32),
-            pltpu.VMEM((SLICE, STATE), F32),
+            pltpu.VMEM((NC // 2, STATE, 2 * CH), BF16),
             pltpu.VMEM((HALF, STATE), BF16),
             pltpu.VMEM((8, CH), F32),
             pltpu.VMEM((GROUP, 8, CH), F32),
             dma, dma, dma, dma, dma, dma, dma, dma, dma, dma, dma, dma,
             dma((LEVELS,)), dma((LEVELS,)), dma, dma, dma((LEVELS,)), dma((LEVELS,)), dma, dma,
+            pltpu.SemaphoreType.REGULAR, pltpu.SemaphoreType.REGULAR,
         ],
         compiler_params=pltpu.CompilerParams(
             collective_id=0, has_side_effects=True, vmem_limit_bytes=50 << 20),

time: 45.9 us -> 39.3 us (0.86)
  Pallas kernels: 44.6 us -> 38 us
    pallas_call x1, Pallas kernels: 44.6 us -> 38 us  [shards(): pl.pallas_call(kernel, out_shape=jax.ShapeDtypeStruct((NC, CH, ROWS), BF1...]
where the time goes in v3:
time: 39.3 us; the launch traced here: 39.2 us
  Pallas kernels  38 us (97%)
  local copies, waits for them, and re-layouts  1.15 us (3%)
    pallas_call x1, Pallas kernels, shards(): pl.pallas_call(kernel, out_shape=jax.ShapeDtypeStruct((NC, CH, ROWS), BF1...  38 us
    unnamed x1, local copies, waits for them, and re-layouts  1.15 us

profile of v3, /device:TPU:30, one launch (start us, length us, event | category | flops | bytes accessed | tf_op | source)
XLA Modules:
  0.0 39.2 jit_solution(7415003857558316444)
XLA Ops:
  0.0 38.0 %layer.1 = bf16[6,128,1024]{2,1,0:T(8,128)(2,1)S(1)} custom-call(bf16[6,128,128]{2,1,0:T(8,128)(2,1)} %bitcast.6, bf16[6,128,128]{2,1,0:T(8,128)(2,1)} %bitcast.7, bf16[6,128,1024]{2,1,0:T(8,128)(2,1)} %bitcast.5, f32[16,768]{1,0:T(8,128)} %ld_hbm.1, bf16[7,16,768]{2,1,0:T(8,128)(2,1)} %lw_hbm.1, f32[16]{0:T(128)} %skip_hbm.1, bf16[1024]{0:T(1024)(128)(2,1)} %gain_hbm.1), custom_call_target="tpu_custom_call" | custom-call | tf_op jit(solution)/shard_map/layer/pallas_call | solution.py:472
  38.0 1.1 %copy.9 = bf16[768,1024]{1,0:T(8,128)(2,1)} copy(bf16[768,1024]{1,0:T(8,128)(2,1)S(1)} %bitcast.4) | data formatting | bytes 3145728

commit v4 on v3

--- a/solution.py
+++ b/solution.py
@@ -25,6 +25,10 @@
 GROUP = 8
 CHANNELS = 8192
 STARTS = {2: 0, 3: 4, 4: 6, 5: 7}
+SIDE = 4
+STEPS = sorted(
+    ((dx, dy) for dx in range(SIDE) for dy in range(SIDE) if dx + dy > 0),
+    key=lambda d: -min(d[0], SIDE - d[0]) - min(d[1], SIDE - d[1]))
 
 
 def rows_of(start, size):
@@ -52,6 +56,12 @@
     def at(s):
         return {"seq": s, "head": head}
 
+    cx = chip % SIDE
+    cy = chip // SIDE
+
+    def away(step):
+        return SIDE * ((cy + step[1]) % SIDE) + (cx + step[0]) % SIDE
+
     def same_core(to):
         return at(base + 2 * to + core)
 
@@ -89,9 +99,8 @@
 
     rank = rank_of(head)
 
-    @pl.loop(1, CHIPS)
-    def _(r):
-        greet(same_core((chip + r) % CHIPS))
+    for step in STEPS:
+        greet(same_core(away(step)))
 
     greet(partner)
 
@@ -221,9 +230,8 @@
     crow_ref[...] = crow
     crows_ref[chip] = crow
 
-    @pl.loop(1, CHIPS)
-    def _(r):
-        to = (chip + r) % CHIPS
+    for step in STEPS:
+        to = away(step)
         remote(pair_ref.at[rows_of(SLICE * to, SLICE)], gath_ref.at[chip], p1_ss, p1_rs,
                same_core(to)).start()
         remote(crow_ref, crows_ref.at[chip], cr_ss, cr_rs, same_core(to)).start()
@@ -235,13 +243,13 @@
     first_level = remote(
         pair_ref, bucket_ref.at[1, half], n1_ss, n1_rs, same_core(chip + 1 - 2 * bits[1]))
 
+    gath_ref[chip] = pair_ref[rows_of(SLICE * chip, SLICE)]
+
+    inside(2, NC)
+
     @pl.when(bits[1] == 0)
     def _():
         first_level.start()
-
-    gath_ref[chip] = pair_ref[rows_of(SLICE * chip, SLICE)]
-
-    inside(2, NC)
 
     fifteen = pl.ds(0, CHIPS - 1)
     crs = remote(crows_ref.at[fifteen], crows_ref.at[fifteen], cr_ss, cr_rs, partner)
@@ -271,9 +279,8 @@
         node_ref.at[STARTS[5]], bucket_ref.at[5, rows_of(mine, SLICE)], z_ss, z_rs, zpeer)
 
     for level in range(2, 5):
-        @pl.loop(1, CHIPS)
-        def _(r):
-            to = (chip + r) % CHIPS
+        for step in STEPS:
+            to = away(step)
 
             @pl.when((to // (1 << (level - 1))) % 2 == 1)
             def _():
@@ -343,18 +350,17 @@
 
     @pl.when(core == 1)
     def _():
-        cross(0, core)
+        cross(0, 1)
         remote(st_ref.at[other], bucket_ref.at[0, other], l0_ss, l0_rs, partner).wait_recv()
-        cross(0, 1 - core)
+        cross(0, 0)
 
     @pl.when(zhi == 1)
     def _():
         up.wait_recv()
         own = bucket_ref.at[5, rows_of(mine, SLICE)]
 
-        @pl.loop(1, CHIPS)
-        def _(r):
-            remote(own, own, p2_ss.at[5], p2_rs.at[5], same_core((chip + r) % CHIPS)).start()
+        for step in STEPS:
+            remote(own, own, p2_ss.at[5], p2_rs.at[5], same_core(away(step))).start()
 
     @pl.when(bits[1] == 1)
     def _():
@@ -364,34 +370,58 @@
         forwarded(1).wait_recv()
         cross(1, 1 - core)
 
-    for level in range(2, 5):
+    def landed(level):
+        slices(level).wait_recv()
+        forward(level).start()
+
+    def rest(level):
+        forwarded(level).wait_recv()
+        cross(level, 1 - core)
+
+    @pl.when(bits[2] == 1)
+    def _():
+        landed(2)
+        cross(2, core)
+
+    @pl.when((bits[2] == 1) & (core == 0))
+    def _():
+        rest(2)
+
+    for level in range(3, 5):
         @pl.when(bits[level] == 1)
         def _():
-            slices(level).wait_recv()
-            forward(level).start()
+            landed(level)
+
+    for level in range(3, 5):
+        @pl.when(bits[level] == 1)
+        def _():
             cross(level, core)
 
-    def rest(level):
+    @pl.when((bits[2] == 1) & (core == 1))
+    def _():
+        rest(2)
+
+    @pl.when(zhi == 1)
+    def _():
+        landed(5)
+        cross(5, core)
+
+    sq_ref[...] = jnp.zeros((8, CH), F32)
+
+    def squares(c, rows):
+        y = acc_ref[c, rows]
+        return jnp.sum(y * y, axis=0, keepdims=True)
+
+    for c in range(NC):
+        sq_ref[c:c + 1] = squares(c, half)
+
+    for level in range(3, LEVELS):
         @pl.when(bits[level] == 1)
         def _():
-            forwarded(level).wait_recv()
-            cross(level, 1 - core)
-
-    rest(2)
-
-    @pl.when(zhi == 1)
-    def _():
-        slices(5).wait_recv()
-        forward(5).start()
-        cross(5, core)
-
-    for level in range(3, LEVELS):
-        rest(level)
-
-    sq_ref[...] = jnp.zeros((8, CH), F32)
-    for c in range(NC):
-        y = acc_ref[c]
-        sq_ref[c:c + 1] = jnp.sum(y * y, axis=0, keepdims=True)
+            rest(level)
+
+    for c in range(NC):
+        sq_ref[c:c + 1] = sq_ref[c:c + 1] + squares(c, other)
     sqs_ref[head] = sq_ref[...]
 
     @pl.when(rank < GROUP - 1)

time: 39.3 us -> 39.2 us (level)
  no operation moved by 1% of the time
where the time goes in v4:
time: 39.2 us; the launch traced here: 39 us
  Pallas kernels  37.9 us (97%)
  local copies, waits for them, and re-layouts  1.15 us (3%)
    pallas_call x1, Pallas kernels, shards(): pl.pallas_call(kernel, out_shape=jax.ShapeDtypeStruct((NC, CH, ROWS), BF1...  37.9 us
    unnamed x1, local copies, waits for them, and re-layouts  1.15 us

profile of v4, /device:TPU:30, one launch (start us, length us, event | category | flops | bytes accessed | tf_op | source)
XLA Modules:
  0.0 39.0 jit_solution(9859182990942351250)
XLA Ops:
  0.0 37.9 %layer.1 = bf16[6,128,1024]{2,1,0:T(8,128)(2,1)S(1)} custom-call(bf16[6,128,128]{2,1,0:T(8,128)(2,1)} %bitcast.6, bf16[6,128,128]{2,1,0:T(8,128)(2,1)} %bitcast.7, bf16[6,128,1024]{2,1,0:T(8,128)(2,1)} %bitcast.5, f32[16,768]{1,0:T(8,128)} %ld_hbm.1, bf16[7,16,768]{2,1,0:T(8,128)(2,1)} %lw_hbm.1, f32[16]{0:T(128)} %skip_hbm.1, bf16[1024]{0:T(1024)(128)(2,1)} %gain_hbm.1), custom_call_target="tpu_custom_call" | custom-call | tf_op jit(solution)/shard_map/layer/pallas_call | solution.py:502
  37.9 1.1 %copy.9 = bf16[768,1024]{1,0:T(8,128)(2,1)} copy(bf16[768,1024]{1,0:T(8,128)(2,1)S(1)} %bitcast.4) | data formatting | bytes 3145728

commit v5 on v4

--- a/solution.py
+++ b/solution.py
@@ -38,7 +38,7 @@
 def kernel(
     q_hbm, k_hbm, v_hbm, ld_hbm, lw_hbm, skip_hbm, gain_hbm, out_ref,
     q_ref, k_ref, v_ref, ld_ref, lw_ref, skip_ref, gain_ref, in_sem,
-    lc_ref, lct_ref, w0_ref, ci_ref, cum_ref, coef_ref, vt_ref, rb_ref, st_ref, acc_ref, y_ref,
+    lc_ref, lct_ref, w0_ref, ci_ref, cum_ref, coef_ref, vt_ref, sc_ref, rb_ref, run_ref, st_ref, acc_ref, y_ref,
     comb_ref, pcomb_ref, fall_ref, pair_ref, crow_ref, crows_ref,
     gath_ref, node_ref, bucket_ref, qt_ref, bb_ref, sq_ref, sqs_ref,
     ex_ss, ex_rs, cb_ss, cb_rs, l0_ss, l0_rs, cr_ss, cr_rs, p1_ss, p1_rs, n1_ss, n1_rs,
@@ -143,30 +143,24 @@
     comb_ref[0:HEADS] = total
     comb_ref[HEADS:HEADS + 8] = jnp.broadcast_to(trow, (8, CH))
 
-    st_ref[...] = jnp.zeros((ROWS, STATE), F32)
     loads[1].wait()
 
     @pl.loop(0, NC)
     def _(c):
         pltpu.make_async_copy(v_hbm.at[c], v_ref.at[c], in_sem.at[6 + c]).wait()
-        lc = lc_ref[c]
-        last = jnp.broadcast_to(lc[:, CH - 1:CH], (HEADS, CH))
-        fall = jnp.exp(last)
-        tail = jnp.exp(last - lc)
-        scaled = []
+        tail = jnp.exp(comb_ref[0:HEADS] - cum_ref[c])
         for j in range(ROWS // CH):
             vt = v_ref[c, :, j * CH:(j + 1) * CH].T
             vt_ref[c, j * CH:(j + 1) * CH, :] = vt
             wide = vt.astype(F32)
             for i in range(2):
                 h = 2 * j + i
-                scaled.append((wide[i * DIM:(i + 1) * DIM] * tail[h:h + 1]).astype(BF16))
-        new = jnp.dot(jnp.concatenate(scaled, axis=0), k_ref[c], preferred_element_type=F32)
-        for h in range(HEADS):
-            rows = slice(h * DIM, (h + 1) * DIM)
-            old = st_ref[rows]
-            rb_ref[c, rows] = old.astype(BF16)
-            st_ref[rows] = fall[h:h + 1] * old + new[rows]
+                sc_ref[c, h * DIM:(h + 1) * DIM] = (
+                    wide[i * DIM:(i + 1) * DIM] * tail[h:h + 1]).astype(BF16)
+
+    st_ref[...] = jnp.dot(
+        jnp.concatenate([sc_ref[c] for c in range(NC)], axis=1),
+        k_ref[...].reshape(TOK, STATE), preferred_element_type=F32)
 
     pl.semaphore_wait(barrier, CHIPS - 1 + 1 + rank + zhi)
 
@@ -214,7 +208,27 @@
                     w0_ref[c, h:h + 1] * o + ci_ref[c, h:h + 1] * inter[rows]
                     + skip_ref[h] * vt.astype(F32))
 
-    inside(0, 2)
+    rb_ref[0] = jnp.zeros((ROWS, STATE), BF16)
+    run_ref[...] = jnp.zeros((ROWS, STATE), F32)
+
+    def prefix(first, last):
+        @pl.loop(first, last)
+        def _(c):
+            lc = lc_ref[c]
+            end = jnp.broadcast_to(lc[:, CH - 1:CH], (HEADS, CH))
+            fall = jnp.exp(end)
+            tail = jnp.exp(end - lc)
+            scaled = [
+                (vt_ref[c, h * DIM:(h + 1) * DIM].astype(F32) * tail[h:h + 1]).astype(BF16)
+                for h in range(HEADS)]
+            new = jnp.dot(jnp.concatenate(scaled, axis=0), k_ref[c], preferred_element_type=F32)
+            for h in range(HEADS):
+                rows = slice(h * DIM, (h + 1) * DIM)
+                state = fall[h:h + 1] * run_ref[rows] + new[rows]
+                run_ref[rows] = state
+                rb_ref[c + 1, rows] = state.astype(BF16)
+
+    prefix(0, 3)
 
     comb.wait_recv()
     remote(st_ref.at[half], bucket_ref.at[0, half], ex_ss, ex_rs, partner).wait_recv()
@@ -245,11 +259,14 @@
 
     gath_ref[chip] = pair_ref[rows_of(SLICE * chip, SLICE)]
 
-    inside(2, NC)
+    prefix(3, NC - 1)
+    inside(0, 3)
 
     @pl.when(bits[1] == 0)
     def _():
         first_level.start()
+
+    inside(3, NC)
 
     fifteen = pl.ds(0, CHIPS - 1)
     crs = remote(crows_ref.at[fifteen], crows_ref.at[fifteen], cr_ss, cr_rs, partner)
@@ -520,7 +537,9 @@
             pltpu.VMEM((NC, HEADS, CH), F32),
             pltpu.VMEM((LEVELS, NC, HEADS, CH), F32),
             pltpu.VMEM((NC, ROWS, CH), BF16),
+            pltpu.VMEM((NC, ROWS, CH), BF16),
             pltpu.VMEM((NC, ROWS, STATE), BF16),
+            pltpu.VMEM((ROWS, STATE), F32),
             pltpu.VMEM((ROWS, STATE), F32),
             pltpu.VMEM((NC, ROWS, CH), F32),
             pltpu.VMEM((NC, CH, ROWS), F32),

time: 39.2 us -> 39.2 us (level)
  no operation moved by 1% of the time
where the time goes in v5:
time: 39.2 us; the launch traced here: 39 us
  Pallas kernels  37.9 us (97%)
  local copies, waits for them, and re-layouts  1.15 us (3%)
    pallas_call x1, Pallas kernels, shards(): pl.pallas_call(kernel, out_shape=jax.ShapeDtypeStruct((NC, CH, ROWS), BF1...  37.9 us
    unnamed x1, local copies, waits for them, and re-layouts  1.15 us

profile of v5, /device:TPU:30, one launch (start us, length us, event | category | flops | bytes accessed | tf_op | source)
XLA Modules:
  0.0 39.0 jit_solution(7602632167354915366)
XLA Ops:
  0.0 37.9 %layer.1 = bf16[6,128,1024]{2,1,0:T(8,128)(2,1)S(1)} custom-call(bf16[6,128,128]{2,1,0:T(8,128)(2,1)} %bitcast.6, bf16[6,128,128]{2,1,0:T(8,128)(2,1)} %bitcast.7, bf16[6,128,1024]{2,1,0:T(8,128)(2,1)} %bitcast.5, f32[16,768]{1,0:T(8,128)} %ld_hbm.1, bf16[7,16,768]{2,1,0:T(8,128)(2,1)} %lw_hbm.1, f32[16]{0:T(128)} %skip_hbm.1, bf16[1024]{0:T(1024)(128)(2,1)} %gain_hbm.1), custom_call_target="tpu_custom_call" | custom-call | tf_op jit(solution)/shard_map/layer/pallas_call | solution.py:519
  37.9 1.1 %copy.9 = bf16[768,1024]{1,0:T(8,128)(2,1)} copy(bf16[768,1024]{1,0:T(8,128)(2,1)S(1)} %bitcast.4) | data formatting | bytes 3145728
